TPU v7x, 256 devices: a whole 4x4x8 slice. The times are simulated.
256 devices in a mesh: section: 2 (over x_lo), tp: 8 (over y, core), ctx: 16 (over x_hi, z).
Axes of the slice: x: 4 (x_hi: 2, x_lo: 2; x = x_hi * 2 + x_lo), y: 4, z: 8, core: 2. Of those that a mesh axis runs over, the one named last changes fastest.
Arguments:
- tokens_in: bfloat16 [2, 32, 16384], P(None, None, 'ctx'), may hold values from -6 to 6
- norm_gain: bfloat16 [2, 16384], P('section', 'ctx'), may hold values from 0.25 to 1.75
- w_qkv: bfloat16 [2, 16384, 18432], P('section', 'ctx', 'tp'), may hold values from -0.375 to 0.375
- w_out: bfloat16 [2, 16384, 16384], P('section', 'tp', 'ctx'), may hold values from -0.046875 to 0.046875
- prefix_keys: bfloat16 [2, 8, 65536, 128], P('section', 'tp', 'ctx'), may hold values from -400 to 400
- prefix_values: bfloat16 [2, 8, 65536, 128], P('section', 'tp', 'ctx'), may hold values from -6 to 6
- suffix_keys: bfloat16 [2, 8, 32, 512, 128], P('section', 'tp', 'ctx'), may hold values from -27 to 27
- suffix_values: bfloat16 [2, 8, 32, 512, 128], P('section', 'tp', 'ctx'), may hold values from -6 to 6
- lengths: int32 [32], replicated, may hold values from 1 to 512, 8192 in all
- order: int32 [32], replicated, may hold values from 0 to 31, each once
Outputs:
- layer_out: float32 [2, 2, 32, 16384], P('section', None, 'tp', 'ctx')
Inputs may be any that keep to these rules, and one draw needn't show every extreme that they name: `lengths`: some sample has 512. `order`: each sample appears in exactly one row.
All inputs are finite; a program needn't handle non-finite values.
Results may differ from a plain program's by a relative error of at most 0.014.
Values may be sent and summed in bfloat16 or wider, within the bound.
A program may use at most 128 MiB of HBM per device.

v0:
```python
import math

import jax
import jax.numpy as jnp
from jax import lax
from jax.sharding import PartitionSpec as P

D = 16384
HD = 128
G = 16


EPSILON = 1e-05
NEGATIVE = -1e30


def in_blocks(value, dim, length):
    lengths = value.shape
    parts = value.reshape(*lengths[:dim], length, lengths[dim] // length, *lengths[dim + 1 :])
    return jnp.moveaxis(parts, dim, 0)


def sum_at_owner(value, axis, dim):
    parts = in_blocks(value, dim, lax.axis_size(axis))
    arrived = lax.all_to_all(parts, axis, split_axis=0, concat_axis=0, tiled=True)
    return arrived.sum(axis=0)


def padded_to(lines, length):
    spare = -lines.shape[0] % length
    if not spare:
        return lines
    return jnp.concatenate([lines, jnp.zeros((spare, *lines.shape[1:]), lines.dtype)])


def in_order(parts, dim):
    lengths = list(parts.shape[1:])
    lengths[dim] *= parts.shape[0]
    return jnp.moveaxis(parts, 0, dim).reshape(lengths)


def copy_for_each(value, axis):
    copies = jnp.broadcast_to(value, (lax.axis_size(axis), *value.shape))
    return lax.all_to_all(copies, axis, split_axis=0, concat_axis=0, tiled=True)


def collect(value, axis, dim):
    return in_order(copy_for_each(value, axis), dim)


def sum_by_parts(value, axes):
    own = sum_at_owner(padded_to(value, lax.axis_size(axes)), axes, 0)
    whole = collect(own, axes, 0)
    return whole[: len(value)].reshape(value.shape)


def in_one(arrays, axis):
    ends = [0]
    for a in arrays:
        ends.append(ends[-1] + a.size)
    subtotal = sum_by_parts(jnp.concatenate([a.ravel() for a in arrays]), axis)
    return tuple((subtotal[b:e].reshape(a.shape) for a, b, e in zip(arrays, ends, ends[1:])))


def side_by_side(arrays, axis, split_dim, concat_dim, along):
    widths = [math.prod(a.shape[along:]) for a in arrays]
    both = jnp.concatenate(
        [a.reshape(*a.shape[:along], w) for a, w in zip(arrays, widths)], axis=along
    )
    filled = lax.all_to_all(both, axis, split_axis=split_dim, concat_axis=concat_dim, tiled=True)
    parts = jnp.split(filled, [sum(widths[:k]) for k in range(1, len(widths))], axis=along)
    return tuple(
        (b.reshape(*filled.shape[:along], *a.shape[along:]) for a, b in zip(arrays, parts))
    )


def from_behind(value, axis, steps):
    count = lax.axis_size(axis)
    initial, last = (max(0, -steps), min(count, count - steps))
    return lax.ppermute(value, axis, [(source, source + steps) for source in range(initial, last)])


def combine(earlier, later):
    first_max, first_sum, first_out = earlier
    second_max, second_sum, second_out = later
    joint_max = jnp.maximum(first_max, second_max)
    first_scale = jnp.exp(first_max - joint_max)
    second_scale = jnp.exp(second_max - joint_max)
    return (
        joint_max,
        first_sum * first_scale + second_sum * second_scale,
        first_out * first_scale[..., None] + second_out * second_scale[..., None],
    )


def rounded(values):
    return lax.optimization_barrier(values.astype(jnp.bfloat16)).astype(jnp.float32)


def finish(joined, queries, keys_new, values_new, keys_old, values_old, old_on):
    row_max, row_sum, row_out = joined
    score_scale = HD ** (-0.5)
    own_scores = (
        jnp.einsum("rjgd,rjd->rjg", queries, keys_new, preferred_element_type=jnp.float32)
        * score_scale
    )
    terms = [(own_scores, values_new)]
    if keys_old is not None:
        old_scores = (
            jnp.einsum("rjgd,rjd->rjg", queries, keys_old, preferred_element_type=jnp.float32)
            * score_scale
        )
        terms.append((jnp.where(old_on, old_scores, NEGATIVE), values_old))
    joint_max = row_max
    for scores, values in terms:
        joint_max = jnp.maximum(joint_max, scores)
    factor = jnp.exp(row_max - joint_max)
    row_sum = row_sum * factor
    row_out = row_out * factor[..., None]
    for scores, values in terms:
        weights = jnp.exp(scores - joint_max)
        row_sum = row_sum + weights
        row_out = row_out + rounded(weights)[..., None] * values.astype(jnp.float32)[:, :, None, :]
    return (row_out / row_sum[..., None]).astype(jnp.bfloat16)


def layer_pass(
    hidden,
    gain,
    qkv_weight,
    out_weight,
    pre_keys,
    pre_values,
    suf_keys,
    suf_values,
    local_lengths,
    row_order,
    first_sample,
    keys_old,
    values_old,
    old_on,
):
    row_count = hidden.shape[0]
    squares = jnp.sum(hidden * hidden, axis=1)
    scaled = (hidden * gain.astype(jnp.float32)[None, :]).astype(jnp.bfloat16)
    partial_proj = jnp.dot(scaled, qkv_weight, preferred_element_type=jnp.float32)
    squares, partial_proj = in_one((squares, partial_proj), "ctx")
    projected = (partial_proj * lax.rsqrt(squares / D + EPSILON)[:, None]).astype(jnp.bfloat16)
    heads_local = projected.shape[1] // ((G + 2) * HD)
    projected = projected.reshape(row_count, heads_local, G + 2, HD)
    queries = projected[:, :, :G]
    keys_new = projected[:, :, G]
    values_new = projected[:, :, G + 1]
    score_scale = HD ** (-0.5)
    prefix_scores = (
        jnp.einsum("rjgd,jpd->rjgp", queries, pre_keys, preferred_element_type=jnp.float32)
        * score_scale
    )
    prefix_max = jnp.max(prefix_scores, axis=3)
    prefix_weights = jnp.exp(prefix_scores - prefix_max[..., None])
    prefix_sum = jnp.sum(prefix_weights, axis=3)
    prefix_out = jnp.einsum(
        "rjgp,jpd->rjgd",
        prefix_weights.astype(jnp.bfloat16),
        pre_values,
        preferred_element_type=jnp.float32,
    )
    sample_slots = suf_keys.shape[1]
    sample_ids = first_sample + jnp.arange(sample_slots, dtype=jnp.int32)
    owners = (row_order[None, :] == sample_ids[:, None]).astype(jnp.float32)
    owned = jnp.sum(owners, axis=0) > 0.5
    local_queries = jnp.einsum(
        "ir,rjgd->ijgd", owners, queries.astype(jnp.float32), precision=lax.Precision.HIGHEST
    ).astype(jnp.bfloat16)
    suffix_scores = (
        jnp.einsum("ijgd,jipd->ijgp", local_queries, suf_keys, preferred_element_type=jnp.float32)
        * score_scale
    )
    in_suffix = (jnp.arange(suf_keys.shape[2], dtype=jnp.int32)[None, :] < local_lengths[:, None])[
        :, None, None, :
    ]
    suffix_max = jnp.max(jnp.where(in_suffix, suffix_scores, NEGATIVE), axis=3)
    suffix_weights = jnp.where(in_suffix, jnp.exp(suffix_scores - suffix_max[..., None]), 0.0)
    suffix_sum = jnp.sum(suffix_weights, axis=3)
    suffix_out = jnp.einsum(
        "ijgp,jipd->ijgd",
        suffix_weights.astype(jnp.bfloat16),
        suf_values,
        preferred_element_type=jnp.float32,
    )
    mapped_max = jnp.where(
        owned[:, None, None],
        jnp.einsum("ir,ijg->rjg", owners, suffix_max, precision=lax.Precision.HIGHEST),
        NEGATIVE,
    )
    mapped_sum = jnp.einsum("ir,ijg->rjg", owners, suffix_sum, precision=lax.Precision.HIGHEST)
    mapped_out = jnp.einsum("ir,ijgd->rjgd", owners, suffix_out, precision=lax.Precision.HIGHEST)
    local = combine((prefix_max, prefix_sum, prefix_out), (mapped_max, mapped_sum, mapped_out))
    all_max, all_sum, all_out = side_by_side(
        (local[0][None], local[1][None], local[2][None]), "ctx", 1, 0, 4
    )
    joint_max = jnp.max(all_max, axis=0)
    factors = jnp.exp(all_max - joint_max[None])
    joined = (
        joint_max,
        jnp.sum(all_sum * factors, axis=0),
        jnp.sum(all_out * factors[..., None], axis=0),
    )
    share = row_count // lax.axis_size("ctx")
    offset = lax.axis_index("ctx") * share

    def rows_here(values):
        if values is None:
            return None
        return lax.dynamic_slice_in_dim(values, offset, share, 0)

    attention_share = finish(
        joined,
        rows_here(queries),
        rows_here(keys_new),
        rows_here(values_new),
        rows_here(keys_old),
        rows_here(values_old),
        old_on,
    )
    attention = collect(attention_share, "ctx", 0)
    head_terms = jnp.dot(
        attention.reshape(row_count, -1), out_weight, preferred_element_type=jnp.float32
    )
    tp_share = row_count // lax.axis_size("tp")
    tp_offset = lax.axis_index("tp") * tp_share
    summed = sum_at_owner(head_terms, "tp", 0)
    passed = lax.dynamic_slice_in_dim(hidden, tp_offset, tp_share, 0) + summed
    return (passed, passed, keys_new, values_new)


def on_device(
    tokens_in,
    norm_gain,
    w_qkv,
    w_out,
    prefix_keys,
    prefix_values,
    suffix_keys,
    suffix_values,
    lengths,
    order,
):
    on_first = lax.axis_index("section") == 0
    groups = 1
    plan = [(step_index, group) for step_index in range(2) for group in range(groups)]
    batch = tokens_in.shape[1]
    row_count = batch // groups
    sample_slots = suffix_keys.shape[2]
    first_sample = lax.axis_index("ctx") * sample_slots
    local_lengths = lax.dynamic_slice_in_dim(lengths, first_sample, sample_slots, 0)
    stored = []
    kept_first = {}
    kept_second = {}
    received = None
    for slot_index in range(len(plan) + 1):
        leading = plan[slot_index] if slot_index < len(plan) else None
        trailing = plan[slot_index - 1] if slot_index >= 1 else None
        if leading is None:
            fresh = jnp.zeros((row_count, tokens_in.shape[2]), jnp.float32)
        else:
            fresh = tokens_in[leading[0]].astype(jnp.float32)
        hidden = fresh if received is None else jnp.where(on_first, fresh, received)
        row_order = jnp.where(on_first, order, order)
        if slot_index >= groups:
            keys_old, values_old = stored[slot_index - groups]
            old_on = jnp.logical_or(on_first, slot_index - 1 >= groups)
        else:
            keys_old, values_old = (None, None)
            old_on = on_first
        passed, kept, keys_new, values_new = layer_pass(
            hidden,
            norm_gain[0],
            w_qkv[0],
            w_out[0],
            prefix_keys[0],
            prefix_values[0],
            suffix_keys[0],
            suffix_values[0],
            local_lengths,
            row_order,
            first_sample,
            keys_old,
            values_old,
            old_on,
        )
        stored.append((keys_new, values_new))
        if leading is not None:
            kept_first[leading] = kept
        if trailing is not None:
            kept_second[trailing] = kept
        if slot_index < len(plan):
            arrived = from_behind(passed, "section", 1)
            received = collect(arrived, "tp", 0)

    def assemble(kept_map):
        step_rows = []
        for step_index in range(2):
            shares = kept_map[step_index, 0]
            step_rows.append(shares)
        return jnp.stack(step_rows)

    result = jnp.where(on_first, assemble(kept_first), assemble(kept_second))
    return result[None]


def solution(mesh):
    in_specs = (
        P(None, None, "ctx"),
        P("section", "ctx"),
        P("section", "ctx", "tp"),
        P("section", "tp", "ctx"),
        P("section", "tp", "ctx", None),
        P("section", "tp", "ctx", None),
        P("section", "tp", "ctx", None, None),
        P("section", "tp", "ctx", None, None),
        P(),
        P(),
    )
    out_specs = P("section", None, "tp", "ctx")
    return jax.shard_map(
        on_device, mesh=mesh, in_specs=in_specs, out_specs=out_specs, check_vma=False
    )
```

profile of v0, /device:TPU:3, one launch (start us, length us, event | category | flops | bytes accessed | tf_op | source)
XLA Modules:
  0.0 379.5 jit_solution(1508201780678283253)
XLA Ops:
  0.0 1.1 multiply_reduce_fusion.2
  1.8 3.3 fusion.13
  5.2 1.1 all_to_all.81
  6.4 9.9 %all-to-all-start = ((f32[16,1,4610]{2,1,0:T(1,128)}), f32[16,1,4610]{2,1,0:T(1,128)S(1)}, u32[]{:S(2)}, u32[]{:S(2)}) async-start(f32[16,1,4610]{2,1,0:T(1,128)} %all_to_all.81), calls=%async_computation | async-start | bytes 606208 | tf_op jit(solution)/shard_map/all_to_all | solution.py:25
  17.0 10.2 %all-to-all-done = f32[16,1,4610]{2,1,0:T(1,128)S(1)} async-done(((f32[16,1,4610]{2,1,0:T(1,128)}), f32[16,1,4610]{2,1,0:T(1,128)S(1)}, u32[]{:S(2)}, u32[]{:S(2)}) %all-to-all-start) | async-done | bytes 295072 | tf_op jit(solution)/shard_map/all_to_all | solution.py:25
  28.3 5.7 %all-to-all-start.1 = ((f32[16,1,4610]{2,1,0:T(1,128)}), f32[16,1,4610]{2,1,0:T(1,128)S(1)}, u32[]{:S(2)}, u32[]{:S(2)}) async-start(f32[16,1,4610]{2,1,0:T(1,128)} %broadcast_in_dim.83), calls=%async_computation.1 | async-start | bytes 606208 | tf_op jit(solution)/shard_map/all_to_all | solution.py:44
  34.3 10.3 %all-to-all-done.1 = f32[16,1,4610]{2,1,0:T(1,128)S(1)} async-done(((f32[16,1,4610]{2,1,0:T(1,128)}), f32[16,1,4610]{2,1,0:T(1,128)S(1)}, u32[]{:S(2)}, u32[]{:S(2)}) %all-to-all-start.1) | async-done | bytes 295072 | tf_op jit(solution)/shard_map/all_to_all | solution.py:44
  47.7 4.5 %bitcast_reduce_fusion.2 = (f32[32,16]{1,0:T(8,128)S(1)}, f32[32,16,4096]{2,1,0:T(8,128)}) fusion(bf16[1,1,4096,128]{3,2,1,0:T(8,128)(2,1)S(1)} %copy-done, bf16[32,1,18,128]{3,2,0,1:T(8,128)(2,1)S(1)} %multiply_convert_fusion.2), kind=kOutput, calls=%fused_computation.7 | convolution fusion | flops 541064704 | bytes 9570304 | tf_op jit(solution)/shard_map/rjgd,jpd->rjgp/dot_general | solution.py:156
  52.6 4.9 %fusion.4 = f32[32,16]{1,0:T(8,128)S(1)} fusion(f32[32,16,4096]{2,1,0:T(8,128)} %get-tuple-element.55, f32[32,16]{1,0:T(8,128)S(1)} %get-tuple-element.54), kind=kLoop, calls=%fused_computation.10 | loop fusion | flops 6290944 | bytes 8392704 | tf_op jit(solution)/shard_map/reduce_sum | solution.py:161
  57.8 0.9 copy.328
  58.7 0.9 copy.327
  59.6 4.9 %fusion.48 = f32[1,32,1,16,128]{4,3,1,2,0:T(8,128)S(1)} fusion(f32[32,16,4096]{2,1,0:T(8,128)} %get-tuple-element.55, f32[32,16]{1,0:T(8,128)S(1)} %get-tuple-element.54, bf16[1,1,4096,128]{3,2,1,0:T(8,128)(2,1)S(1)} %copy-done.1, f32[32,16,128]{2,0,1:T(8,128)S(1)} %fusion.143, f32[32,16]{1,0:T(8,128)S(1)} %copy.325, f32[32,16]{1,0:T(8,128)S(1)} %copy.323), kind=kOutput, calls=%fused_computation.39 | convolution fusion | flops 543358976 | bytes 9967616 | tf_op jit(solution)/shard_map/rjgp,jpd->rjgd/dot_general | solution.py:162
  64.6 1.1 maximum_bitcast_fusion
  65.7 5.9 %all-to-all-start.2 = ((f32[1,32,1,16,130]{4,3,2,0,1:T(8,128)}), f32[1,32,1,16,130]{4,3,2,0,1:T(8,128)S(1)}, u32[]{:S(2)}, u32[]{:S(2)}) async-start(f32[1,32,1,16,130]{4,3,2,0,1:T(8,128)} %maximum_bitcast_fusion), calls=%async_computation.2 | async-start | bytes 1048576 | tf_op jit(solution)/shard_map/all_to_all | solution.py:70
  72.2 1.4 fusion.153
  73.6 12.2 %all-to-all-done.2 = f32[1,32,1,16,130]{4,3,2,0,1:T(8,128)S(1)} async-done(((f32[1,32,1,16,130]{4,3,2,0,1:T(8,128)}), f32[1,32,1,16,130]{4,3,2,0,1:T(8,128)S(1)}, u32[]{:S(2)}, u32[]{:S(2)}) %all-to-all-start.2) | async-done | bytes 266272 | tf_op jit(solution)/shard_map/all_to_all | solution.py:70
  86.7 1.8 copy.332
  93.2 6.4 %all-to-all-start.3 = ((bf16[16,2,1,16,128]{4,3,1,2,0:T(8,128)(2,1)}), bf16[16,2,1,16,128]{4,3,1,2,0:T(8,128)(2,1)S(1)}, u32[]{:S(2)}, u32[]{:S(2)}) async-start(bf16[16,2,1,16,128]{4,3,1,2,0:T(8,128)(2,1)} %broadcast_in_dim.161), calls=%async_computation.3 | async-start | bytes 262144 | tf_op jit(solution)/shard_map/all_to_all | solution.py:44
  99.5 9.0 %all-to-all-done.3 = bf16[16,2,1,16,128]{4,3,1,2,0:T(8,128)(2,1)S(1)} async-done(((bf16[16,2,1,16,128]{4,3,1,2,0:T(8,128)(2,1)}), bf16[16,2,1,16,128]{4,3,1,2,0:T(8,128)(2,1)S(1)}, u32[]{:S(2)}, u32[]{:S(2)}) %all-to-all-start.3) | async-done | bytes 131104 | tf_op jit(solution)/shard_map/all_to_all | solution.py:44
  108.6 3.6 fusion.22
  112.2 7.8 %all-to-all-start.4 = ((f32[8,4,1024]{2,1,0:T(4,128)}), f32[8,4,1024]{2,1,0:T(4,128)S(1)}, u32[]{:S(2)}, u32[]{:S(2)}) async-start(f32[8,4,1024]{2,1,0:T(4,128)} %fusion.22), calls=%async_computation.4 | async-start | bytes 262144 | tf_op jit(solution)/shard_map/all_to_all | solution.py:25
  120.7 4.5 %all-to-all-done.4 = f32[8,4,1024]{2,1,0:T(4,128)S(1)} async-done(((f32[8,4,1024]{2,1,0:T(4,128)}), f32[8,4,1024]{2,1,0:T(4,128)S(1)}, u32[]{:S(2)}, u32[]{:S(2)}) %all-to-all-start.4) | async-done | bytes 131104 | tf_op jit(solution)/shard_map/all_to_all | solution.py:25
  125.3 1.3 collective-permute-start
  126.6 3.2 collective-permute-done
  130.5 5.3 %all-to-all-start.5 = ((f32[8,4,1024]{2,1,0:T(4,128)}), f32[8,4,1024]{2,1,0:T(4,128)S(1)}, u32[]{:S(2)}, u32[]{:S(2)}) async-start(f32[8,4,1024]{2,1,0:T(4,128)} %broadcast_in_dim.162), calls=%async_computation.5 | async-start | bytes 262144 | tf_op jit(solution)/shard_map/all_to_all | solution.py:44
  135.8 5.2 %all-to-all-done.5 = f32[8,4,1024]{2,1,0:T(4,128)S(1)} async-done(((f32[8,4,1024]{2,1,0:T(4,128)}), f32[8,4,1024]{2,1,0:T(4,128)S(1)}, u32[]{:S(2)}, u32[]{:S(2)}) %all-to-all-start.5) | async-done | bytes 131104 | tf_op jit(solution)/shard_map/all_to_all | solution.py:44
  141.7 3.2 fusion.11
  145.7 1.1 pad_maximum_fusion.1
  147.2 13.3 %all_to_all.121 = f32[16,1,4610]{2,1,0:T(1,128)S(1)} all-to-all(f32[16,1,4610]{2,1,0:T(1,128)S(1)} %all_to_all.89), channel_id=1, replica_groups=mesh['section'=2,'tp'=8,'ctx'=16] {'ctx'}, dimensions={0} | all-to-all | bytes 590080 | tf_op jit(solution)/shard_map/all_to_all | solution.py:25
  160.9 16.4 %all_to_all.122 = f32[16,1,4610]{2,1,0:T(1,128)S(1)} all-to-all(f32[16,1,4610]{2,1,0:T(1,128)S(1)} %broadcast_in_dim.163), channel_id=1, replica_groups=mesh['section'=2,'tp'=8,'ctx'=16] {'ctx'}, dimensions={0} | all-to-all | bytes 590080 | tf_op jit(solution)/shard_map/all_to_all | solution.py:44
  179.0 1.0 reshape.843
  181.6 4.5 %bitcast_reduce_fusion.1 = (f32[32,16]{1,0:T(8,128)S(1)}, f32[32,16,4096]{2,1,0:T(8,128)}) fusion(bf16[1,1,4096,128]{3,2,1,0:T(8,128)(2,1)S(1)} %copy-done, bf16[32,1,18,128]{3,2,0,1:T(8,128)(2,1)S(1)} %multiply_convert_fusion.1), kind=kOutput, calls=%fused_computation.4 | convolution fusion | flops 541064704 | bytes 9570304 | tf_op jit(solution)/shard_map/rjgd,jpd->rjgp/dot_general | solution.py:156
  186.9 4.9 %fusion.6 = f32[32,16]{1,0:T(8,128)S(1)} fusion(f32[32,16,4096]{2,1,0:T(8,128)} %get-tuple-element.59, f32[32,16]{1,0:T(8,128)S(1)} %get-tuple-element.58), kind=kLoop, calls=%fused_computation.12 | loop fusion | flops 6290944 | bytes 8392704 | tf_op jit(solution)/shard_map/reduce_sum | solution.py:161
  192.1 0.9 copy.346
  193.9 4.9 %fusion.60 = f32[1,32,1,16,128]{4,3,1,2,0:T(8,128)S(1)} fusion(f32[32,16,4096]{2,1,0:T(8,128)} %get-tuple-element.59, f32[32,16]{1,0:T(8,128)S(1)} %get-tuple-element.58, bf16[1,1,4096,128]{3,2,1,0:T(8,128)(2,1)S(1)} %copy-done.1, f32[32,16,128]{2,0,1:T(8,128)S(1)} %fusion.141, f32[32,16]{1,0:T(8,128)S(1)} %copy.343, f32[32,16]{1,0:T(8,128)S(1)} %copy.341), kind=kOutput, calls=%fused_computation.43 | convolution fusion | flops 543358976 | bytes 9967616 | tf_op jit(solution)/shard_map/rjgp,jpd->rjgd/dot_general | solution.py:162
  198.8 1.1 maximum_bitcast_fusion.1
  200.0 5.9 %all-to-all-start.8 = ((f32[1,32,1,16,130]{4,3,2,0,1:T(8,128)}), f32[1,32,1,16,130]{4,3,2,0,1:T(8,128)S(1)}, u32[]{:S(2)}, u32[]{:S(2)}) async-start(f32[1,32,1,16,130]{4,3,2,0,1:T(8,128)} %maximum_bitcast_fusion.1), calls=%async_computation.8 | async-start | bytes 1048576 | tf_op jit(solution)/shard_map/all_to_all | solution.py:70
  207.6 12.5 %all-to-all-done.8 = f32[1,32,1,16,130]{4,3,2,0,1:T(8,128)S(1)} async-done(((f32[1,32,1,16,130]{4,3,2,0,1:T(8,128)}), f32[1,32,1,16,130]{4,3,2,0,1:T(8,128)S(1)}, u32[]{:S(2)}, u32[]{:S(2)}) %all-to-all-start.8) | async-done | bytes 266272 | tf_op jit(solution)/shard_map/all_to_all | solution.py:70
  220.1 0.9 fusion.220
  221.0 1.2 copy.350
  222.3 1.2 copy.389
  223.9 15.2 %all_to_all.123 = bf16[16,2,1,16,128]{4,3,1,2,0:T(8,128)(2,1)S(1)} all-to-all(bf16[16,2,1,16,128]{4,3,1,2,0:T(8,128)(2,1)S(1)} %broadcast_in_dim.166), channel_id=1, replica_groups=mesh['section'=2,'tp'=8,'ctx'=16] {'ctx'}, dimensions={0} | all-to-all | bytes 262144 | tf_op jit(solution)/shard_map/all_to_all | solution.py:44
  239.1 3.6 fusion.20
  242.8 6.6 %all-to-all-start.10 = ((f32[8,4,1024]{2,1,0:T(4,128)}), f32[8,4,1024]{2,1,0:T(4,128)S(1)}, u32[]{:S(2)}, u32[]{:S(2)}) async-start(f32[8,4,1024]{2,1,0:T(4,128)} %fusion.20), calls=%async_computation.10 | async-start | bytes 262144 | tf_op jit(solution)/shard_map/all_to_all | solution.py:25
  249.4 5.2 %all-to-all-done.10 = f32[8,4,1024]{2,1,0:T(4,128)S(1)} async-done(((f32[8,4,1024]{2,1,0:T(4,128)}), f32[8,4,1024]{2,1,0:T(4,128)S(1)}, u32[]{:S(2)}, u32[]{:S(2)}) %all-to-all-start.10) | async-done | bytes 131104 | tf_op jit(solution)/shard_map/all_to_all | solution.py:25
  255.4 1.3 collective-permute-start.1
  256.7 3.2 collective-permute-done.1
  259.9 9.6 %all_to_all.124 = f32[8,4,1024]{2,1,0:T(4,128)S(1)} all-to-all(f32[8,4,1024]{2,1,0:T(4,128)S(1)} %broadcast_in_dim.168), channel_id=1, replica_groups=mesh['section'=2,'tp'=8,'ctx'=16] {'tp'}, dimensions={0} | all-to-all | bytes 262144 | tf_op jit(solution)/shard_map/all_to_all | solution.py:44
  269.8 3.2 fusion.9
  273.8 1.1 pad_maximum_fusion.2
  275.4 13.3 %all_to_all.125 = f32[16,1,4610]{2,1,0:T(1,128)S(1)} all-to-all(f32[16,1,4610]{2,1,0:T(1,128)S(1)} %all_to_all.97), channel_id=1, replica_groups=mesh['section'=2,'tp'=8,'ctx'=16] {'ctx'}, dimensions={0} | all-to-all | bytes 590080 | tf_op jit(solution)/shard_map/all_to_all | solution.py:25
  289.0 16.4 %all_to_all.126 = f32[16,1,4610]{2,1,0:T(1,128)S(1)} all-to-all(f32[16,1,4610]{2,1,0:T(1,128)S(1)} %broadcast_in_dim.169), channel_id=1, replica_groups=mesh['section'=2,'tp'=8,'ctx'=16] {'ctx'}, dimensions={0} | all-to-all | bytes 590080 | tf_op jit(solution)/shard_map/all_to_all | solution.py:44
  307.2 1.0 reshape.852
  309.1 4.5 %bitcast_reduce_fusion = (f32[32,16]{1,0:T(8,128)S(1)}, f32[32,16,4096]{2,1,0:T(8,128)}) fusion(bf16[1,1,4096,128]{3,2,1,0:T(8,128)(2,1)S(1)} %copy-done, bf16[32,1,18,128]{3,2,0,1:T(8,128)(2,1)S(1)} %multiply_convert_fusion), kind=kOutput, calls=%fused_computation.1 | convolution fusion | flops 541064704 | bytes 9570304 | tf_op jit(solution)/shard_map/rjgd,jpd->rjgp/dot_general | solution.py:156
  314.4 4.9 %fusion.8 = f32[32,16]{1,0:T(8,128)S(1)} fusion(f32[32,16,4096]{2,1,0:T(8,128)} %get-tuple-element.63, f32[32,16]{1,0:T(8,128)S(1)} %get-tuple-element.62), kind=kLoop, calls=%fused_computation.14 | loop fusion | flops 6290944 | bytes 8392704 | tf_op jit(solution)/shard_map/reduce_sum | solution.py:161
  319.8 0.9 copy.363
  320.7 4.9 %fusion.72 = f32[1,32,1,16,128]{4,3,1,2,0:T(8,128)S(1)} fusion(f32[32,16,4096]{2,1,0:T(8,128)} %get-tuple-element.63, f32[32,16]{1,0:T(8,128)S(1)} %get-tuple-element.62, bf16[1,1,4096,128]{3,2,1,0:T(8,128)(2,1)S(1)} %copy-done.1, f32[32,16,128]{2,0,1:T(8,128)S(1)} %fusion.139, f32[32,16]{1,0:T(8,128)S(1)} %copy.361, f32[32,16]{1,0:T(8,128)S(1)} %copy.359), kind=kOutput, calls=%fused_computation.47 | convolution fusion | flops 543358976 | bytes 9967616 | tf_op jit(solution)/shard_map/rjgp,jpd->rjgd/dot_general | solution.py:162
  325.6 1.1 maximum_bitcast_fusion.2
  326.8 5.9 %all-to-all-start.14 = ((f32[1,32,1,16,130]{4,3,2,0,1:T(8,128)}), f32[1,32,1,16,130]{4,3,2,0,1:T(8,128)S(1)}, u32[]{:S(2)}, u32[]{:S(2)}) async-start(f32[1,32,1,16,130]{4,3,2,0,1:T(8,128)} %maximum_bitcast_fusion.2), calls=%async_computation.14 | async-start | bytes 1048576 | tf_op jit(solution)/shard_map/all_to_all | solution.py:70
  333.6 13.6 %all-to-all-done.14 = f32[1,32,1,16,130]{4,3,2,0,1:T(8,128)S(1)} async-done(((f32[1,32,1,16,130]{4,3,2,0,1:T(8,128)}), f32[1,32,1,16,130]{4,3,2,0,1:T(8,128)S(1)}, u32[]{:S(2)}, u32[]{:S(2)}) %all-to-all-start.14) | async-done | bytes 266272 | tf_op jit(solution)/shard_map/all_to_all | solution.py:70
  348.3 14.9 %all_to_all.127 = bf16[16,2,1,16,128]{4,3,1,2,0:T(8,128)(2,1)S(1)} all-to-all(bf16[16,2,1,16,128]{4,3,1,2,0:T(8,128)(2,1)S(1)} %broadcast_in_dim.171), channel_id=1, replica_groups=mesh['section'=2,'tp'=8,'ctx'=16] {'ctx'}, dimensions={0} | all-to-all | bytes 262144 | tf_op jit(solution)/shard_map/all_to_all | solution.py:44
  363.2 3.6 fusion.18
  366.9 6.6 %all-to-all-start.16 = ((f32[8,4,1024]{2,1,0:T(4,128)}), f32[8,4,1024]{2,1,0:T(4,128)S(1)}, u32[]{:S(2)}, u32[]{:S(2)}) async-start(f32[8,4,1024]{2,1,0:T(4,128)} %fusion.18), calls=%async_computation.16 | async-start | bytes 262144 | tf_op jit(solution)/shard_map/all_to_all | solution.py:25
  373.5 5.2 %all-to-all-done.16 = f32[8,4,1024]{2,1,0:T(4,128)S(1)} async-done(((f32[8,4,1024]{2,1,0:T(4,128)}), f32[8,4,1024]{2,1,0:T(4,128)S(1)}, u32[]{:S(2)}, u32[]{:S(2)}) %all-to-all-start.16) | async-done | bytes 131104 | tf_op jit(solution)/shard_map/all_to_all | solution.py:25
  (195 shorter events, 33.2 us)
Async XLA Ops:
  0.0 47.7 %copy-start = (bf16[1,1,4096,128]{3,2,1,0:T(8,128)(2,1)S(1)}, bf16[1,1,4096,128]{3,2,1,0:T(8,128)(2,1)}, u32[]{:S(2)}) copy-start(bf16[1,1,4096,128]{3,2,1,0:T(8,128)(2,1)} %param.14) | copy-start | bytes 3145732
  0.0 34.1 %copy-start.18 = (s32[32]{0:T(128)S(1)}, s32[32]{0:T(128)}, u32[]{:S(2)}) copy-start(s32[32]{0:T(128)} %param.19) | copy-start | bytes 388
  0.0 34.0 %copy-start.17 = (s32[32]{0:T(128)S(1)}, s32[32]{0:T(128)}, u32[]{:S(2)}) copy-start(s32[32]{0:T(128)} %param.18) | copy-start | bytes 388
  0.0 46.6 %copy-start.2 = (bf16[1,1,2,512,128]{4,3,2,1,0:T(8,128)(2,1)S(1)}, bf16[1,1,2,512,128]{4,3,2,1,0:T(8,128)(2,1)}, u32[]{:S(2)}) copy-start(bf16[1,1,2,512,128]{4,3,2,1,0:T(8,128)(2,1)} %param.16) | copy-start | bytes 786436
  0.0 47.1 %copy-start.3 = (bf16[1,1,2,512,128]{4,3,2,1,0:T(8,128)(2,1)S(1)}, bf16[1,1,2,512,128]{4,3,2,1,0:T(8,128)(2,1)}, u32[]{:S(2)}) copy-start(bf16[1,1,2,512,128]{4,3,2,1,0:T(8,128)(2,1)} %param.17) | copy-start | bytes 786436
  6.4 20.8 %all-to-all-start = ((f32[16,1,4610]{2,1,0:T(1,128)}), f32[16,1,4610]{2,1,0:T(1,128)S(1)}, u32[]{:S(2)}, u32[]{:S(2)}) async-start(f32[16,1,4610]{2,1,0:T(1,128)} %all_to_all.81), calls=%async_computation | async-start | bytes 606208 | tf_op jit(solution)/shard_map/all_to_all | solution.py:25
  16.3 41.3 %copy-start.21 = (s32[2]{0:T(128)}, s32[2]{0:T(128)S(1)}, u32[]{:S(2)}) copy-start(s32[2]{0:T(128)S(1)} %iota_add_fusion) | copy-start | bytes 28
  28.3 16.3 %all-to-all-start.1 = ((f32[16,1,4610]{2,1,0:T(1,128)}), f32[16,1,4610]{2,1,0:T(1,128)S(1)}, u32[]{:S(2)}, u32[]{:S(2)}) async-start(f32[16,1,4610]{2,1,0:T(1,128)} %broadcast_in_dim.83), calls=%async_computation.1 | async-start | bytes 606208 | tf_op jit(solution)/shard_map/all_to_all | solution.py:44
  34.0 18.6 %copy-start.26 = (pred[32]{0:T(512)(128)(4,1)}, pred[32]{0:T(512)(128)(4,1)S(1)}, u32[]{:S(2)}) copy-start(pred[32]{0:T(512)(128)(4,1)S(1)} %broadcast_compare_fusion) | copy-start | bytes 100
  47.7 11.9 %copy-start.1 = (bf16[1,1,4096,128]{3,2,1,0:T(8,128)(2,1)S(1)}, bf16[1,1,4096,128]{3,2,1,0:T(8,128)(2,1)}, u32[]{:S(2)}) copy-start(bf16[1,1,4096,128]{3,2,1,0:T(8,128)(2,1)} %param.15) | copy-start | bytes 3145732
  59.6 4.9 %copy-start.6 = (f32[1,32,1,16,1]{4,3,1,2,0:T(8,128)S(1)}, f32[1,32,1,16,1]{4,3,1,2,0:T(8,128)}, u32[]{:S(2)}) copy-start(f32[1,32,1,16,1]{4,3,1,2,0:T(8,128)} %copy.328) | copy-start | bytes 6148
  59.6 5.0 %copy-start.8 = (f32[1,32,1,16,1]{4,3,1,2,0:T(8,128)S(1)}, f32[1,32,1,16,1]{4,3,1,2,0:T(8,128)}, u32[]{:S(2)}) copy-start(f32[1,32,1,16,1]{4,3,1,2,0:T(8,128)} %copy.327) | copy-start | bytes 6148
  59.6 60.4 %copy-start.11 = (bf16[2,32,1024]{2,1,0:T(8,128)(2,1)S(1)}, bf16[2,32,1024]{2,1,0:T(8,128)(2,1)}, u32[]{:S(2)}) copy-start(bf16[2,32,1024]{2,1,0:T(8,128)(2,1)} %param.10) | copy-start | bytes 393220
  65.7 20.1 %all-to-all-start.2 = ((f32[1,32,1,16,130]{4,3,2,0,1:T(8,128)}), f32[1,32,1,16,130]{4,3,2,0,1:T(8,128)S(1)}, u32[]{:S(2)}, u32[]{:S(2)}) async-start(f32[1,32,1,16,130]{4,3,2,0,1:T(8,128)} %maximum_bitcast_fusion), calls=%async_computation.2 | async-start | bytes 1048576 | tf_op jit(solution)/shard_map/all_to_all | solution.py:70
  71.6 14.2 %copy-start.14 = (bf16[32,1,1,128]{3,2,0,1:T(2,128)(2,1)}, bf16[32,1,1,128]{3,2,0,1:T(2,128)(2,1)S(1)}, u32[]{:S(2)}) copy-start(bf16[32,1,1,128]{3,2,0,1:T(2,128)(2,1)S(1)} %get-tuple-element.33) | copy-start | bytes 24580
  93.2 15.4 %all-to-all-start.3 = ((bf16[16,2,1,16,128]{4,3,1,2,0:T(8,128)(2,1)}), bf16[16,2,1,16,128]{4,3,1,2,0:T(8,128)(2,1)S(1)}, u32[]{:S(2)}, u32[]{:S(2)}) async-start(bf16[16,2,1,16,128]{4,3,1,2,0:T(8,128)(2,1)} %broadcast_in_dim.161), calls=%async_computation.3 | async-start | bytes 262144 | tf_op jit(solution)/shard_map/all_to_all | solution.py:44
  112.2 13.0 %all-to-all-start.4 = ((f32[8,4,1024]{2,1,0:T(4,128)}), f32[8,4,1024]{2,1,0:T(4,128)S(1)}, u32[]{:S(2)}, u32[]{:S(2)}) async-start(f32[8,4,1024]{2,1,0:T(4,128)} %fusion.22), calls=%async_computation.4 | async-start | bytes 262144 | tf_op jit(solution)/shard_map/all_to_all | solution.py:25
  125.3 19.6 %copy-start.12 = (f32[4,1024]{1,0:T(4,128)}, f32[4,1024]{1,0:T(4,128)S(1)}, u32[]{:S(2)}) copy-start(f32[4,1024]{1,0:T(4,128)S(1)} %bitcast_add_fusion) | copy-start | bytes 49156
  125.3 4.5 %collective-permute-start = (f32[4,1024]{1,0:T(4,128)S(1)}, f32[4,1024]{1,0:T(4,128)S(1)}, u32[]{:S(2)}, u32[]{:S(2)}) collective-permute-start(f32[4,1024]{1,0:T(4,128)S(1)} %bitcast_add_fusion), channel_id=1, source_target_pairs={{0,128},{1,129},{2,130},{3,131},{4,132},{5,133},{6,134},{7,135},{8... | collective-permute-start | bytes 49160 | tf_op jit(solution)/shard_map/ppermute | solution.py:80
  130.5 10.6 %all-to-all-start.5 = ((f32[8,4,1024]{2,1,0:T(4,128)}), f32[8,4,1024]{2,1,0:T(4,128)S(1)}, u32[]{:S(2)}, u32[]{:S(2)}) async-start(f32[8,4,1024]{2,1,0:T(4,128)} %broadcast_in_dim.162), calls=%async_computation.5 | async-start | bytes 262144 | tf_op jit(solution)/shard_map/all_to_all | solution.py:44
  141.0 0.7 copy-start.4
  146.8 39.7 %copy-start.19 = (s32[32]{0:T(128)S(1)}, s32[32]{0:T(128)}, u32[]{:S(2)}) copy-start(s32[32]{0:T(128)} %param.19) | copy-start | bytes 388
  146.8 39.7 %copy-start.22 = (s32[2]{0:T(128)S(1)}, s32[2]{0:T(128)}, u32[]{:S(2)}) copy-start(s32[2]{0:T(128)} %copy-done.21) | copy-start | bytes 28
  146.8 39.7 %copy-start.27 = (pred[32]{0:T(512)(128)(4,1)S(1)}, pred[32]{0:T(512)(128)(4,1)}, u32[]{:S(2)}) copy-start(pred[32]{0:T(512)(128)(4,1)} %copy-done.26) | copy-start | bytes 100
  181.6 10.2 %copy-start.23 = (s32[2]{0:T(128)S(1)}, s32[2]{0:T(128)}, u32[]{:S(2)}) copy-start(s32[2]{0:T(128)} %copy-done.21) | copy-start | bytes 28
  191.8 32.0 %copy-start.16 = (f32[2,1,1,128]{3,2,0,1:T(1,128)S(1)}, f32[2,1,1,128]{3,2,0,1:T(1,128)}, u32[]{:S(2)}) copy-start(f32[2,1,1,128]{3,2,0,1:T(1,128)} %fusion.178) | copy-start | bytes 3076
  193.9 4.9 %copy-start.7 = (f32[1,32,1,16,1]{4,3,1,2,0:T(8,128)S(1)}, f32[1,32,1,16,1]{4,3,1,2,0:T(8,128)}, u32[]{:S(2)}) copy-start(f32[1,32,1,16,1]{4,3,1,2,0:T(8,128)} %copy.346) | copy-start | bytes 6148
  193.9 5.0 %copy-start.9 = (f32[1,32,1,16,1]{4,3,1,2,0:T(8,128)S(1)}, f32[1,32,1,16,1]{4,3,1,2,0:T(8,128)}, u32[]{:S(2)}) copy-start(f32[1,32,1,16,1]{4,3,1,2,0:T(8,128)} %copy.345) | copy-start | bytes 6148
  193.9 55.5 %copy-start.5 = (f32[8,4,1024]{2,1,0:T(4,128)S(1)}, f32[8,4,1024]{2,1,0:T(4,128)}, u32[]{:S(2)}) copy-start(f32[8,4,1024]{2,1,0:T(4,128)} %copy-done.4) | copy-start | bytes 393220
  200.0 20.1 %all-to-all-start.8 = ((f32[1,32,1,16,130]{4,3,2,0,1:T(8,128)}), f32[1,32,1,16,130]{4,3,2,0,1:T(8,128)S(1)}, u32[]{:S(2)}, u32[]{:S(2)}) async-start(f32[1,32,1,16,130]{4,3,2,0,1:T(8,128)} %maximum_bitcast_fusion.1), calls=%async_computation.8 | async-start | bytes 1048576 | tf_op jit(solution)/shard_map/all_to_all | solution.py:70
  205.9 16.3 %copy-start.15 = (bf16[32,1,1,128]{3,2,0,1:T(2,128)(2,1)}, bf16[32,1,1,128]{3,2,0,1:T(2,128)(2,1)S(1)}, u32[]{:S(2)}) copy-start(bf16[32,1,1,128]{3,2,0,1:T(2,128)(2,1)S(1)} %get-tuple-element.29) | copy-start | bytes 24580
  242.8 11.9 %all-to-all-start.10 = ((f32[8,4,1024]{2,1,0:T(4,128)}), f32[8,4,1024]{2,1,0:T(4,128)S(1)}, u32[]{:S(2)}, u32[]{:S(2)}) async-start(f32[8,4,1024]{2,1,0:T(4,128)} %fusion.20), calls=%async_computation.10 | async-start | bytes 262144 | tf_op jit(solution)/shard_map/all_to_all | solution.py:25
  255.4 4.5 %collective-permute-start.1 = (f32[4,1024]{1,0:T(4,128)S(1)}, f32[4,1024]{1,0:T(4,128)S(1)}, u32[]{:S(2)}, u32[]{:S(2)}) collective-permute-start(f32[4,1024]{1,0:T(4,128)S(1)} %fusion.129), channel_id=1, source_target_pairs={{0,128},{1,129},{2,130},{3,131},{4,132},{5,133},{6,134},{7,135},{8... | collective-permute-start | bytes 49160 | tf_op jit(solution)/shard_map/ppermute | solution.py:80
  274.9 39.1 %copy-start.20 = (s32[32]{0:T(128)S(1)}, s32[32]{0:T(128)}, u32[]{:S(2)}) copy-start(s32[32]{0:T(128)} %param.19) | copy-start | bytes 388
  274.9 39.1 %copy-start.24 = (s32[2]{0:T(128)S(1)}, s32[2]{0:T(128)}, u32[]{:S(2)}) copy-start(s32[2]{0:T(128)} %copy-done.21) | copy-start | bytes 28
  274.9 39.1 %copy-start.28 = (pred[32]{0:T(512)(128)(4,1)S(1)}, pred[32]{0:T(512)(128)(4,1)}, u32[]{:S(2)}) copy-start(pred[32]{0:T(512)(128)(4,1)} %copy-done.26) | copy-start | bytes 100
  309.1 10.2 %copy-start.25 = (s32[2]{0:T(128)S(1)}, s32[2]{0:T(128)}, u32[]{:S(2)}) copy-start(s32[2]{0:T(128)} %copy-done.21) | copy-start | bytes 28
  320.7 4.9 %copy-start.10 = (f32[1,32,1,16,1]{4,3,1,2,0:T(8,128)S(1)}, f32[1,32,1,16,1]{4,3,1,2,0:T(8,128)}, u32[]{:S(2)}) copy-start(f32[1,32,1,16,1]{4,3,1,2,0:T(8,128)} %copy.363) | copy-start | bytes 6148
  320.7 58.1 %copy-start.13 = (f32[4,1024]{1,0:T(4,128)S(1)}, f32[4,1024]{1,0:T(4,128)}, u32[]{:S(2)}) copy-start(f32[4,1024]{1,0:T(4,128)} %copy-done.12) | copy-start | bytes 49156
  326.8 20.4 %all-to-all-start.14 = ((f32[1,32,1,16,130]{4,3,2,0,1:T(8,128)}), f32[1,32,1,16,130]{4,3,2,0,1:T(8,128)S(1)}, u32[]{:S(2)}, u32[]{:S(2)}) async-start(f32[1,32,1,16,130]{4,3,2,0,1:T(8,128)} %maximum_bitcast_fusion.2), calls=%async_computation.14 | async-start | bytes 1048576 | tf_op jit(solution)/shard_map/all_to_all | solution.py:70
  366.9 11.9 %all-to-all-start.16 = ((f32[8,4,1024]{2,1,0:T(4,128)}), f32[8,4,1024]{2,1,0:T(4,128)S(1)}, u32[]{:S(2)}, u32[]{:S(2)}) async-start(f32[8,4,1024]{2,1,0:T(4,128)} %fusion.18), calls=%async_computation.16 | async-start | bytes 262144 | tf_op jit(solution)/shard_map/all_to_all | solution.py:25
where the time goes:
time: 382 us; the launch traced here: 379 us
  blocking collectives  99 us (26%)
  waiting for transfers between devices  94.6 us (25%)
  starting transfers between devices  68.5 us (18%)
  matrix products  57 us (15%)
  other arithmetic  35.4 us (9%)
  local copies, waits for them, and re-layouts  24.1 us (6%)
    all_to_all x5, blocking collectives, copy_for_each(): return lax.all_to_all(copies, axis, split_axis=0, concat_axis=0, tiled=True)  72.4 us
    all_to_all x3, waiting for transfers between devices, side_by_side(): lax.all_to_all(both, axis, split_axis=split_dim, concat_axis=concat_dim,...  38.4 us
    all_to_all x4, starting transfers between devices, sum_at_owner(): lax.all_to_all(parts, axis, split_axis=0, concat_axis=0, tiled=True)  30.9 us
    all_to_all x2, blocking collectives, sum_at_owner(): lax.all_to_all(parts, axis, split_axis=0, concat_axis=0, tiled=True)  26.6 us
    all_to_all x4, waiting for transfers between devices, sum_at_owner(): lax.all_to_all(parts, axis, split_axis=0, concat_axis=0, tiled=True)  25.2 us
    all_to_all x3, waiting for transfers between devices, copy_for_each(): return lax.all_to_all(copies, axis, split_axis=0, concat_axis=0, tiled=True)  24.6 us
    all_to_all x3, starting transfers between devices, side_by_side(): lax.all_to_all(both, axis, split_axis=split_dim, concat_axis=concat_dim,...  17.7 us
    all_to_all x3, starting transfers between devices, copy_for_each(): return lax.all_to_all(copies, axis, split_axis=0, concat_axis=0, tiled=True)  17.4 us
  transfers between devices with their start and end apart: 12, of which 12 were waited for; matrix products, arithmetic and copies ran while one was open for 2% of the time, Pallas kernels for 0%

commit v1 on v0

v1 whole, which is shorter than its diff:
```python
import functools
import math

import jax
import jax.numpy as jnp
from jax import lax
from jax.experimental import pallas as pl
from jax.experimental.pallas import tpu as pltpu
from jax.sharding import PartitionSpec as P

HD = 128
LANES = 128
STEPS = 2
EPSILON = 1e-05
NEGATIVE = -1e30
SCALE2 = HD ** (-0.5) * math.log2(math.e)
HEADS_PER_BLOCK = 4
F32 = jnp.float32
BF16 = jnp.bfloat16


def iota(shape, dim):
    return lax.broadcasted_iota(jnp.int32, shape, dim)


def column_to_row(column):
    rows = column.shape[0]
    picked = jnp.where(iota((rows, LANES), 0) == iota((rows, LANES), 1), column, 0.0)
    return jnp.sum(picked, axis=0, keepdims=True)


def row_to_column(row, rows):
    spread = jnp.broadcast_to(row, (rows, LANES))
    picked = jnp.where(iota((rows, LANES), 0) == iota((rows, LANES), 1), spread, 0.0)
    return jnp.sum(picked, axis=1, keepdims=True)


def in_three(row):
    high = row.astype(BF16).astype(F32)
    rest = row - high
    middle = rest.astype(BF16).astype(F32)
    low = rest - middle
    which = iota((8, LANES), 0)
    block = jnp.where(which == 0, jnp.broadcast_to(high, (8, LANES)), 0.0)
    block = jnp.where(which == 1, jnp.broadcast_to(middle, (8, LANES)), block)
    return jnp.where(which == 2, jnp.broadcast_to(low, (8, LANES)), block)


def kernel(
    nc,
    nt,
    tokens,
    gain,
    w_qkv,
    w_out,
    pre_keys,
    pre_values,
    suf_keys,
    suf_values,
    lengths,
    order,
    out,
    tok_v,
    gain_v,
    gain_next,
    wq_v,
    wo_v,
    k_v,
    vx,
    xg,
    x_res,
    ssb,
    p1,
    r1,
    scales,
    p2,
    r2,
    order_v,
    new_bias,
    s_v,
    p3,
    r3,
    p4,
    a4,
    p5,
    r5,
    xg6,
    ss6,
    xn6,
    load_sem,
    wq_sem,
    send_c,
    recv_c,
    send_t,
    recv_t,
    send_x,
    recv_x,
    send_g,
    recv_g,
):
    sec = lax.axis_index("section")
    tp = lax.axis_index("tp")
    ctx = lax.axis_index("ctx")
    rows = 8 * nt
    heads = nc
    model = wq_v.shape[0]
    prefix = pre_keys.shape[2]
    slots, smax = suf_keys.shape[2], suf_keys.shape[3]
    width = wo_v.shape[1]
    features = model * nc
    new_at = prefix + slots * smax
    tiles = wq_sem.shape[0]

    def load(source, target, k):
        return pltpu.make_async_copy(source, target, load_sem.at[k])

    def load_wq(n):
        cols = pl.ds(n * 256, 256)
        return pltpu.make_async_copy(
            w_qkv.at[0, :, cols], wq_v.at[:, cols], wq_sem.at[n]
        )

    barrier = pltpu.get_barrier_semaphore()

    def greet_ctx(k, carry):
        pl.semaphore_signal(barrier, inc=1, device_id={"ctx": lax.rem(ctx + k, nc)})
        return carry

    def greet_tp(k, carry):
        pl.semaphore_signal(barrier, inc=1, device_id={"tp": lax.rem(tp + k, nt)})
        return carry

    def greet_section(k, carry):
        pl.semaphore_signal(barrier, inc=1, device_id={"section": 1 - sec, "tp": k})
        return carry

    lax.fori_loop(1, nc, greet_ctx, 0)
    lax.fori_loop(1, nt, greet_tp, 0)
    lax.fori_loop(0, nt, greet_section, 0)

    loads = [
        load(tokens, tok_v, 0),
        load(gain, gain_v, 1),
    ]
    for copy in loads:
        copy.start()
    for n in [tiles - 1] + list(range(tiles - 1)):
        load_wq(n).start()
    later = [
        load(pre_keys.at[0, 0], k_v.at[pl.ds(0, prefix)], 2),
        load(pre_values.at[0, 0], vx.at[pl.ds(0, prefix), pl.ds(0, HD)], 3),
    ]
    for i in range(slots):
        at = pl.ds(prefix + i * smax, smax)
        later.append(load(suf_keys.at[0, 0, i], k_v.at[at], 4 + 2 * i))
        later.append(load(suf_values.at[0, 0, i], vx.at[at, pl.ds(0, HD)], 5 + 2 * i))
    out_load = load(w_out.at[0], wo_v, 4 + 2 * slots)
    for copy in later:
        copy.start()
    out_load.start()

    vx[:, HD:] = jnp.ones((vx.shape[0], HD), BF16)
    spare = k_v.shape[0] - new_at - rows
    k_v[pl.ds(new_at + rows, spare), :] = jnp.zeros((spare, HD), BF16)
    vx[pl.ds(new_at + rows, spare), pl.ds(0, HD)] = jnp.zeros((spare, HD), BF16)
    row_of = iota((rows, LANES), 0)
    lane_of = iota((rows, LANES), 1)
    batch_row = ((row_of >> 3) << 2) + (row_of & 3)
    sample = jnp.zeros((rows, LANES), jnp.int32)
    for r in range(rows // STEPS):
        sample = jnp.where(batch_row == r, order[r], sample)
    second = (row_of & 4) == 4
    mine = (row_of & (nc - 1)) == ctx
    allowed = mine & ((lane_of == row_of) | (second & (lane_of == row_of - 4)))
    bias = jnp.where(allowed, 0.0, NEGATIVE)
    for hh in range(HEADS_PER_BLOCK):
        order_v[pl.ds(hh * rows, rows), :] = sample
        new_bias[pl.ds(hh * rows, rows), :] = bias

    for copy in loads:
        copy.wait()

    @pl.when(sec == 0)
    def _():
        g = gain_v[...].astype(F32)
        for j in range(nt):
            x8 = jnp.concatenate(
                [tok_v[t, pl.ds(4 * j, 4), :].astype(F32) for t in range(STEPS)], axis=0
            )
            xg[j] = (x8 * g).astype(BF16)
            total = jnp.sum(x8 * x8, axis=1, keepdims=True)
            ssb[j] = jnp.broadcast_to(total, (8, LANES))

            @pl.when(tp == j)
            def _():
                x_res[...] = x8

    pl.semaphore_wait(barrier, nc - 1 + nt - 1 + nt)

    gain_copy = pltpu.make_async_remote_copy(
        src_ref=gain_v,
        dst_ref=gain_next,
        send_sem=send_g,
        recv_sem=recv_g,
        device_id={"section": 1 - sec},
    )

    def row_copies(k):
        return [
            pltpu.make_async_remote_copy(
                src_ref=xg6,
                dst_ref=xg.at[tp],
                send_sem=send_x.at[0, k],
                recv_sem=recv_x.at[0, tp],
                device_id={"section": 1 - sec, "tp": k},
            ),
            pltpu.make_async_remote_copy(
                src_ref=ss6,
                dst_ref=ssb.at[tp],
                send_sem=send_x.at[1, k],
                recv_sem=recv_x.at[1, tp],
                device_id={"section": 1 - sec, "tp": k},
            ),
        ]

    def row_arrivals(j):
        return [
            pltpu.make_async_remote_copy(
                src_ref=xg.at[j],
                dst_ref=xg.at[j],
                send_sem=send_x.at[0, j],
                recv_sem=recv_x.at[0, j],
                device_id={"section": 1 - sec, "tp": j},
            ),
            pltpu.make_async_remote_copy(
                src_ref=ssb.at[j],
                dst_ref=ssb.at[j],
                send_sem=send_x.at[1, j],
                recv_sem=recv_x.at[1, j],
                device_id={"section": 1 - sec, "tp": j},
            ),
        ]

    rest_copy = pltpu.make_async_remote_copy(
        src_ref=xn6,
        dst_ref=x_res,
        send_sem=send_x.at[2, 0],
        recv_sem=recv_x.at[2, 0],
        device_id={"section": 1 - sec},
    )

    @pl.when(sec == 1)
    def _():
        gain_copy.start()

        def arrive(j, carry):
            for copy in row_arrivals(j):
                copy.wait_recv()
            return carry

        lax.fori_loop(0, nt, arrive, 0)
        gain_copy.wait_send()

    def exchange(phase, source, target):
        def send(d):
            return pltpu.make_async_remote_copy(
                src_ref=source(d),
                dst_ref=target(ctx),
                send_sem=send_c.at[phase, d],
                recv_sem=recv_c.at[phase, ctx],
                device_id={"ctx": d},
            )

        def arrival(d):
            return pltpu.make_async_remote_copy(
                src_ref=target(d),
                dst_ref=target(d),
                send_sem=send_c.at[phase, d],
                recv_sem=recv_c.at[phase, d],
                device_id={"ctx": d},
            )

        def start_all():
            def start(k, carry):
                send(lax.rem(ctx + k, nc)).start()
                return carry

            lax.fori_loop(1, nc, start, 0)

        def wait_all():
            def wait(k, carry):
                arrival(lax.rem(ctx + k, nc)).wait_recv()
                return carry

            lax.fori_loop(1, nc, wait, 0)

        def drain():
            def wait(k, carry):
                send(lax.rem(ctx + k, nc)).wait_send()
                return carry

            lax.fori_loop(1, nc, wait, 0)

        return send, start_all, wait_all, drain

    _, start1, wait1, drain1 = exchange(0, lambda d: p1.at[d], lambda d: r1.at[d])
    xgv = xg[...].reshape(rows, model)
    squares = in_three(column_to_row(ssb[...].reshape(rows, LANES)))
    load_wq(tiles - 1).wait()
    kv = jnp.dot(xgv, wq_v[:, (tiles - 1) * 256 :], preferred_element_type=F32)
    for j in range(nt):
        for part in range(2):
            block = kv[8 * j : 8 * j + 8, part * HD : (part + 1) * HD]
            p1[part * nt + j, pl.ds(rows, 16), :] = jnp.concatenate(
                [block, squares], axis=0
            ).astype(BF16)
    for n in range(tiles - 1):
        load_wq(n).wait()
        two = jnp.dot(xgv, wq_v[:, n * 256 : n * 256 + 256], preferred_element_type=F32)
        p1[2 * n, pl.ds(0, rows), :] = two[:, :HD].astype(BF16)
        p1[2 * n + 1, pl.ds(0, rows), :] = two[:, HD:].astype(BF16)
    start1()
    r1[ctx] = p1[ctx]

    _, start2, wait2, drain2 = exchange(1, lambda d: p2, lambda d: r2.at[d])
    wait1()
    total = r1[0].astype(F32)
    for d in range(1, nc):
        total = total + r1[d].astype(F32)
    square_row = jnp.sum(total[rows + 8 :], axis=0, keepdims=True)
    scale_row = lax.rsqrt(square_row / features + EPSILON)
    scale = row_to_column(scale_row, rows)
    scales[...] = jnp.broadcast_to(scale, (rows, LANES))
    kv_scale = scales[pl.ds(pl.multiple_of(8 * lax.rem(ctx, nt), 8), 8), :]
    done = jnp.concatenate(
        [total[:rows] * scale, total[rows : rows + 8] * kv_scale], axis=0
    ).astype(BF16)
    p2[...] = done
    r2[ctx] = done
    start2()

    send3, _, wait3, drain3 = exchange(2, lambda d: p3.at[d], lambda d: r3.at[d])
    for copy in later:
        copy.wait()
    wait2()
    for j in range(nt // 2):
        at = pl.ds(new_at + 16 * j, 16)
        for part, target in ((0, k_v), (1, vx)):
            pair = [r2[part * nt + 2 * j + i, pl.ds(rows, 8), :].astype(F32) for i in range(2)]
            target[at, pl.ds(0, HD)] = jnp.concatenate(pair, axis=0).astype(BF16)

    block_rows = HEADS_PER_BLOCK * rows
    blocks = heads // HEADS_PER_BLOCK
    chunk = min(512, smax)
    per_block = blocks * ctx // nc

    def scores(queries, start, length):
        return lax.dot_general(
            queries,
            k_v[pl.ds(start, length), :],
            (((1,), (1,)), ((), ())),
            preferred_element_type=F32,
        )

    def lane_max(best, values):
        for n in range(values.shape[1] // LANES):
            best = jnp.maximum(best, values[:, n * LANES : (n + 1) * LANES])
        return best

    def attend(b, carry):
        block = lax.rem(b + per_block, blocks)
        first = block * HEADS_PER_BLOCK
        queries = r2[pl.ds(first, HEADS_PER_BLOCK), pl.ds(0, rows), :].reshape(block_rows, HD)
        best = jnp.where(
            new_bias[...] == 0.0, scores(queries, new_at, LANES), NEGATIVE
        )
        s_v[:, new_at:] = best
        for i in range(slots):
            held = order_v[:, 0:1] == slots * ctx + i
            filled = lengths[slots * ctx + i]
            for n in range(smax // chunk):
                start = prefix + i * smax + n * chunk
                inside = iota((block_rows, chunk), 1) + n * chunk < filled
                values = jnp.where(held & inside, scores(queries, start, chunk), NEGATIVE)
                s_v[:, start : start + chunk] = values
                best = lane_max(best, values)
        for n in range(prefix // chunk):
            values = scores(queries, n * chunk, chunk)
            s_v[:, n * chunk : (n + 1) * chunk] = values
            best = lane_max(best, values)
        top = jnp.max(best, axis=1, keepdims=True)
        sums = jnp.zeros((block_rows, 2 * HD), F32)
        starts = [n * chunk for n in range(new_at // chunk)] + [new_at]
        for start in starts:
            length = chunk if start < new_at else LANES
            weights = jnp.exp2((s_v[:, start : start + length] - top) * SCALE2)
            sums = sums + jnp.dot(
                weights.astype(BF16),
                vx[pl.ds(start, length), :],
                preferred_element_type=F32,
            )
        weight_sum = sums[:, HD:]
        part = sums[:, :HD] / weight_sum
        level = top * SCALE2 + jnp.log2(weight_sum)
        for hh in range(HEADS_PER_BLOCK):
            at = slice(hh * rows, (hh + 1) * rows)
            head = first + hh
            p3[head] = jnp.concatenate(
                [part[at], in_three(column_to_row(level[at]))], axis=0
            ).astype(BF16)

            @pl.when(head != ctx)
            def _():
                send3(head).start()

        return carry

    lax.fori_loop(0, blocks, attend, 0)
    r3[ctx] = p3[ctx]

    def columns(d):
        return a4.at[:, pl.ds(pl.multiple_of(d * HD, HD), HD)]

    _, start4, wait4, drain4 = exchange(3, lambda d: p4, columns)
    wait3()
    levels = jnp.concatenate(
        [
            jnp.sum(r3[d, pl.ds(rows, 8), :].astype(F32), axis=0, keepdims=True)
            for d in range(nc)
        ],
        axis=0,
    )
    factors = jnp.exp2(levels - jnp.max(levels, axis=0, keepdims=True))
    factors = factors / jnp.sum(factors, axis=0, keepdims=True)
    padded = jnp.concatenate([factors, jnp.zeros((LANES - nc, LANES), F32)], axis=0)
    by_row = padded.T[:rows]
    joined = jnp.zeros((rows, HD), F32)
    for d in range(nc):
        joined = joined + by_row[:, d : d + 1] * r3[d, pl.ds(0, rows), :].astype(F32)
    attention = joined.astype(BF16)
    p4[...] = attention
    a4[:, pl.ds(pl.multiple_of(ctx * HD, HD), HD)] = attention
    start4()

    out_load.wait()
    wait4()
    whole = a4[...]
    for n in range(width // 256):
        terms = jnp.dot(whole, wo_v[:, n * 256 : n * 256 + 256], preferred_element_type=F32)
        p5[:, :, n * 256 : n * 256 + 256] = terms.reshape(nt, 8, 256).astype(BF16)

    def term_copy(d):
        return pltpu.make_async_remote_copy(
            src_ref=p5.at[d],
            dst_ref=r5.at[tp],
            send_sem=send_t.at[d],
            recv_sem=recv_t.at[tp],
            device_id={"tp": d},
        )

    def term_arrival(d):
        return pltpu.make_async_remote_copy(
            src_ref=r5.at[d],
            dst_ref=r5.at[d],
            send_sem=send_t.at[d],
            recv_sem=recv_t.at[d],
            device_id={"tp": d},
        )

    def start_terms(k, carry):
        term_copy(lax.rem(tp + k, nt)).start()
        return carry

    def wait_terms(k, carry):
        term_arrival(lax.rem(tp + k, nt)).wait_recv()
        return carry

    lax.fori_loop(1, nt, start_terms, 0)
    r5[tp] = p5[tp]

    @pl.when(sec == 1)
    def _():
        rest_copy.wait_recv()

    lax.fori_loop(1, nt, wait_terms, 0)
    passed = r5[0].astype(F32)
    for d in range(1, nt):
        passed = passed + r5[d].astype(F32)
    passed = passed + x_res[...]

    @pl.when(sec == 0)
    def _():
        gain_copy.wait_recv()
        xg6[...] = (passed * gain_next[...].astype(F32)).astype(BF16)
        total6 = jnp.sum(passed * passed, axis=1, keepdims=True)
        ss6[...] = jnp.broadcast_to(total6, (8, LANES))
        xn6[...] = passed

        def start(k, carry):
            for copy in row_copies(lax.rem(tp + k, nt)):
                copy.start()
            return carry

        lax.fori_loop(0, nt, start, 0)
        rest_copy.start()

    for t in range(STEPS):
        out[0, t] = passed[4 * t : 4 * t + 4]

    drain1()
    drain2()
    drain3()
    drain4()

    def drain_terms(k, carry):
        term_copy(lax.rem(tp + k, nt)).wait_send()
        return carry

    lax.fori_loop(1, nt, drain_terms, 0)

    @pl.when(sec == 0)
    def _():
        def wait(k, carry):
            for copy in row_copies(lax.rem(tp + k, nt)):
                copy.wait_send()
            return carry

        lax.fori_loop(0, nt, wait, 0)
        rest_copy.wait_send()


def on_device(nc, nt, tokens, gain, w_qkv, w_out, pre_k, pre_v, suf_k, suf_v, lengths, order):
    rows = 8 * nt
    model, wide = w_qkv.shape[1:]
    deep, width = w_out.shape[1:]
    prefix = pre_k.shape[2]
    slots, smax = suf_k.shape[2:4]
    keys = prefix + slots * smax + LANES
    block_rows = HEADS_PER_BLOCK * rows
    vmem, dma = pltpu.VMEM, pltpu.SemaphoreType.DMA
    anywhere = pl.BlockSpec(memory_space=pl.ANY)
    scalars = pl.BlockSpec(memory_space=pltpu.SMEM)
    return pl.pallas_call(
        functools.partial(kernel, nc, nt),
        out_shape=jax.ShapeDtypeStruct((1, STEPS, rows // STEPS // nt, width), F32),
        in_specs=[anywhere] * 8 + [scalars] * 2,
        out_specs=pl.BlockSpec(memory_space=pltpu.VMEM),
        scratch_shapes=[
            vmem(tokens.shape, BF16),
            vmem((1, model), BF16),
            vmem((1, model), BF16),
            vmem((model, wide), BF16),
            vmem((deep, width), BF16),
            vmem((keys, HD), BF16),
            vmem((keys, 2 * HD), BF16),
            vmem((nt, 8, model), BF16),
            vmem((8, width), F32),
            vmem((nt, 8, LANES), F32),
            vmem((nc, rows + 16, HD), BF16),
            vmem((nc, rows + 16, HD), BF16),
            vmem((rows, LANES), F32),
            vmem((rows + 8, HD), BF16),
            vmem((nc, rows + 8, HD), BF16),
            vmem((block_rows, LANES), jnp.int32),
            vmem((block_rows, LANES), F32),
            vmem((block_rows, keys), F32),
            vmem((nc, rows + 8, HD), BF16),
            vmem((nc, rows + 8, HD), BF16),
            vmem((rows, HD), BF16),
            vmem((rows, nc * HD), BF16),
            vmem((nt, 8, width), BF16),
            vmem((nt, 8, width), BF16),
            vmem((8, width), BF16),
            vmem((8, LANES), F32),
            vmem((8, width), F32),
            dma((5 + 2 * slots,)),
            dma((wide // 256,)),
            dma((4, nc)),
            dma((4, nc)),
            dma((nt,)),
            dma((nt,)),
            dma((3, nt)),
            dma((3, nt)),
            dma,
            dma,
        ],
        compiler_params=pltpu.CompilerParams(
            collective_id=0, has_side_effects=True, vmem_limit_bytes=60 * 1024 * 1024
        ),
    )(tokens, gain, w_qkv, w_out, pre_k, pre_v, suf_k, suf_v, lengths, order)


def solution(mesh):
    nc, nt = mesh.shape["ctx"], mesh.shape["tp"]
    in_specs = (
        P(None, None, "ctx"),
        P("section", "ctx"),
        P("section", "ctx", "tp"),
        P("section", "tp", "ctx"),
        P("section", "tp", "ctx", None),
        P("section", "tp", "ctx", None),
        P("section", "tp", "ctx", None, None),
        P("section", "tp", "ctx", None, None),
        P(),
        P(),
    )
    return jax.shard_map(
        functools.partial(on_device, nc, nt),
        mesh=mesh,
        in_specs=in_specs,
        out_specs=P("section", None, "tp", "ctx"),
        check_vma=False,
    )
```

time: 382 us -> 131 us (0.34)
  Pallas kernels: 0 us -> 130 us
  blocking collectives: 99 us -> 0 us
  waiting for transfers between devices: 94.6 us -> 0 us
  starting transfers between devices: 68.5 us -> 0 us
  matrix products: 57 us -> 0 us
  other arithmetic: 35.4 us -> 0 us
  local copies, waits for them, and re-layouts: 24.1 us -> 1.38 us
    pallas_call x0 -> x1, Pallas kernels: none -> 130 us  [on_device(): pl.pallas_call(functools.partial(kernel, nc, nt), out_shape=jax.ShapeDtyp...]
    all_to_all x7 -> x0, blocking collectives: 99 us -> none  [the longest x5 72.4 us: copy_for_each(): return lax.all_to_all(copies, axis, split_axis=0, concat_axis=0, tiled=True)]
    all_to_all x10 -> x0, waiting for transfers between devices: 88.2 us -> none  [the longest x3 38.4 us: side_by_side(): lax.all_to_all(both, axis, split_axis=split_dim, concat_axis=concat_dim,...]
    all_to_all x10 -> x0, starting transfers between devices: 65.9 us -> none  [the longest x4 30.9 us: sum_at_owner(): lax.all_to_all(parts, axis, split_axis=0, concat_axis=0, tiled=True)]
    dot_general x35 -> x0, matrix products: 57 us -> none  [the longest x3 14.8 us: layer_pass(): jnp.einsum('rjgp,jpd->rjgd', prefix_weights.astype(jnp.bfloat16), pre_val...]
    reduce_sum x22 -> x0, other arithmetic: 19.3 us -> none  [the longest x3 14.6 us: layer_pass(): prefix_sum = jnp.sum(prefix_weights, axis=3)]
    ppermute x2 -> x0, waiting for transfers between devices: 6.37 us -> none  [from_behind(): lax.ppermute(value, axis, [(source, source + steps) for source in range(i...]
    concatenate x6 -> x0, other arithmetic: 5.74 us -> none  [the longest x3 3.41 us: side_by_side(): jnp.concatenate([a.reshape(*a.shape[:along], w) for a, w in zip(arrays, w...]
  transfers between devices with their start and end apart: 12 -> 0, of which waited for: 12 -> 0; matrix products, arithmetic and copies ran while one was open for 2% -> 0% of each run, Pallas kernels for 0% -> 0%
where the time goes in v1:
time: 131 us
  Pallas kernels  130 us (99%)
  local copies, waits for them, and re-layouts  1.38 us (1%)
    pallas_call x1, Pallas kernels, on_device(): pl.pallas_call(functools.partial(kernel, nc, nt), out_shape=jax.ShapeDtyp...  130 us

profile of v1, /device:TPU:3, one launch (start us, length us, event | category | flops | bytes accessed | tf_op | source)
XLA Modules:
  0.0 131.3 jit_solution(14447352596219876398)
XLA Ops:
  0.0 129.9 %shard_map.100 = f32[1,2,4,1024]{3,2,1,0:T(4,128)} custom-call(bf16[2,32,1024]{2,1,0:T(8,128)(2,1)} %tokens.1, bf16[1,1024]{1,0:T(2,128)(2,1)} %gain.1, bf16[1,1024,2304]{2,1,0:T(8,128)(2,1)} %w_qkv.1, bf16[1,2048,1024]{2,1,0:T(8,128)(2,1)} %w_out.1, bf16[1,1,4096,128]{3,2,1,0:T(8,128)(2,1)} %pre_keys.1, bf16[1,1,4096,128]{3,2,1,0:T(8,128)(2,1)} %pre_values.1, ...), custom_call_target="tpu_custom_call" | custom-call | tf_op jit(solution)/shard_map/pallas_call | solution.py:543
  129.9 1.4 %copy.12 = f32[1,2,4,1024]{3,2,1,0:T(4,128)} copy(f32[1,2,4,1024]{3,2,1,0:T(4,128)} %shard_map.100) | data formatting | bytes 65536

commit v2 on v1

v2 whole, which is shorter than its diff:
```python
import functools
import math

import jax
import jax.numpy as jnp
from jax import lax
from jax.experimental import pallas as pl
from jax.experimental.pallas import tpu as pltpu
from jax.sharding import PartitionSpec as P

HD = 128
LANES = 128
STEPS = 2
EPSILON = 1e-05
NEGATIVE = -1e30
SCALE2 = HD ** (-0.5) * math.log2(math.e)
HEADS_PER_BLOCK = 8
CHUNKS = 2
CHUNK = 512
STRETCH = 2048
F32 = jnp.float32
BF16 = jnp.bfloat16


def iota(shape, dim):
    return lax.broadcasted_iota(jnp.int32, shape, dim)


def column_to_row(column):
    rows = column.shape[0]
    picked = jnp.where(iota((rows, LANES), 0) == iota((rows, LANES), 1), column, 0.0)
    return jnp.sum(picked, axis=0, keepdims=True)


def row_to_column(row, rows):
    spread = jnp.broadcast_to(row, (rows, LANES))
    picked = jnp.where(iota((rows, LANES), 0) == iota((rows, LANES), 1), spread, 0.0)
    return jnp.sum(picked, axis=1, keepdims=True)


def in_three(row):
    high = row.astype(BF16).astype(F32)
    rest = row - high
    middle = rest.astype(BF16).astype(F32)
    low = rest - middle
    which = iota((8, LANES), 0)
    block = jnp.where(which == 0, jnp.broadcast_to(high, (8, LANES)), 0.0)
    block = jnp.where(which == 1, jnp.broadcast_to(middle, (8, LANES)), block)
    return jnp.where(which == 2, jnp.broadcast_to(low, (8, LANES)), block)


def kernel(
    nc,
    nt,
    tokens,
    gain,
    w_qkv,
    w_out,
    pre_keys,
    pre_values,
    suf_keys,
    suf_values,
    lengths,
    order,
    out,
    tok_v,
    gain_v,
    gain_next,
    wq_v,
    wo_v,
    k_v,
    vx,
    xg,
    x_res,
    ssb,
    p1,
    r1,
    p2,
    r2,
    order_v,
    new_bias,
    s_v,
    best_v,
    p3,
    r3,
    p4,
    a4,
    p5,
    r5,
    xg6,
    ss6,
    xn6,
    load_sem,
    wq_sem,
    send_c,
    recv_c,
    send_t,
    recv_t,
    send_x,
    recv_x,
    send_g,
    recv_g,
):
    sec = lax.axis_index("section")
    tp = lax.axis_index("tp")
    ctx = lax.axis_index("ctx")
    rows = 8 * nt
    owners = nt // CHUNKS
    crows = rows // CHUNKS
    half = nc // 2
    heads = nc
    heads_at_once = min(HEADS_PER_BLOCK, heads)

    def slot(j):
        return j % CHUNKS * owners + j // CHUNKS

    tp_chunk = lax.rem(tp, CHUNKS)
    tp_slot = tp_chunk * owners + tp // CHUNKS
    model = wq_v.shape[0]
    prefix = pre_keys.shape[2]
    slots, smax = suf_keys.shape[2], suf_keys.shape[3]
    width = wo_v.shape[1]
    features = model * nc
    new_at = prefix + slots * smax
    tiles = wq_sem.shape[0]

    def load(source, target, k):
        return pltpu.make_async_copy(source, target, load_sem.at[k])

    def load_wq(n):
        cols = pl.ds(n * 256, 256)
        return pltpu.make_async_copy(
            w_qkv.at[0, :, cols], wq_v.at[:, cols], wq_sem.at[n]
        )

    barrier = pltpu.get_barrier_semaphore()

    def greet_ctx(k, carry):
        pl.semaphore_signal(barrier, inc=1, device_id={"ctx": lax.rem(ctx + k, nc)})
        return carry

    def greet_tp(k, carry):
        pl.semaphore_signal(barrier, inc=1, device_id={"tp": lax.rem(tp + k, nt)})
        return carry

    def greet_section(k, carry):
        pl.semaphore_signal(barrier, inc=1, device_id={"section": 1 - sec, "tp": k})
        return carry

    lax.fori_loop(1, nc, greet_ctx, 0)
    lax.fori_loop(1, nt, greet_tp, 0)
    lax.fori_loop(0, nt, greet_section, 0)

    loads = [
        load(tokens, tok_v, 0),
        load(gain, gain_v, 1),
    ]
    for copy in loads:
        copy.start()
    for n in [tiles - 1] + list(range(tiles - 1)):
        load_wq(n).start()
    later = [
        load(pre_keys.at[0, 0], k_v.at[pl.ds(0, prefix)], 2),
        load(pre_values.at[0, 0], vx.at[pl.ds(0, prefix), pl.ds(0, HD)], 3),
    ]
    for i in range(slots):
        at = pl.ds(prefix + i * smax, smax)
        later.append(load(suf_keys.at[0, 0, i], k_v.at[at], 4 + 2 * i))
        later.append(load(suf_values.at[0, 0, i], vx.at[at, pl.ds(0, HD)], 5 + 2 * i))
    out_load = load(w_out.at[0], wo_v, 4 + 2 * slots)
    for copy in later:
        copy.start()
    out_load.start()

    vx[:, HD:] = jnp.ones((vx.shape[0], HD), BF16)
    spare = LANES - crows
    for q in range(CHUNKS):
        at = pl.ds(new_at + q * LANES + crows, spare)
        k_v[at, :] = jnp.zeros((spare, HD), BF16)
        vx[at, pl.ds(0, HD)] = jnp.zeros((spare, HD), BF16)
    row_of = iota((crows, LANES), 0)
    lane_of = iota((crows, LANES), 1)
    batch_row = ((row_of >> 3) << 2) + (row_of & 3)
    second = (row_of & 4) == 4
    mine = (row_of & (nc - 1)) == ctx
    allowed = mine & ((lane_of == row_of) | (second & (lane_of == row_of - 4)))
    bias = jnp.where(allowed, 0.0, NEGATIVE)
    for q in range(CHUNKS):
        sample = jnp.zeros((crows, LANES), jnp.int32)
        for r in range(4 * owners):
            sample = jnp.where(batch_row == r, order[4 * (CHUNKS * (r // 4) + q) + r % 4], sample)
        for hh in range(heads):
            order_v[q, pl.ds(hh * crows, crows), :] = sample
    for hh in range(heads):
        new_bias[pl.ds(hh * crows, crows), :] = bias

    for copy in loads:
        copy.wait()

    @pl.when(sec == 0)
    def _():
        g = gain_v[...].astype(F32)
        for j in range(nt):
            x8 = jnp.concatenate(
                [tok_v[t, pl.ds(4 * j, 4), :].astype(F32) for t in range(STEPS)], axis=0
            )
            xg[slot(j)] = (x8 * g).astype(BF16)
            total = jnp.sum(x8 * x8, axis=1, keepdims=True)
            ssb[slot(j)] = jnp.broadcast_to(total, (8, LANES))

            @pl.when(tp == j)
            def _():
                x_res[...] = x8

    gain_copy = pltpu.make_async_remote_copy(
        src_ref=gain_v,
        dst_ref=gain_next,
        send_sem=send_g,
        recv_sem=recv_g,
        device_id={"section": 1 - sec},
    )

    def row_copies(k):
        return [
            pltpu.make_async_remote_copy(
                src_ref=xg6,
                dst_ref=xg.at[tp_slot],
                send_sem=send_x.at[0, k],
                recv_sem=recv_x.at[0, tp_slot],
                device_id={"section": 1 - sec, "tp": k},
            ),
            pltpu.make_async_remote_copy(
                src_ref=ss6,
                dst_ref=ssb.at[tp_slot],
                send_sem=send_x.at[1, k],
                recv_sem=recv_x.at[1, tp_slot],
                device_id={"section": 1 - sec, "tp": k},
            ),
        ]

    def row_arrivals(j):
        return [
            pltpu.make_async_remote_copy(
                src_ref=xg.at[j],
                dst_ref=xg.at[j],
                send_sem=send_x.at[0, j],
                recv_sem=recv_x.at[0, j],
                device_id={"section": 1 - sec, "tp": j},
            ),
            pltpu.make_async_remote_copy(
                src_ref=ssb.at[j],
                dst_ref=ssb.at[j],
                send_sem=send_x.at[1, j],
                recv_sem=recv_x.at[1, j],
                device_id={"section": 1 - sec, "tp": j},
            ),
        ]

    rest_copy = pltpu.make_async_remote_copy(
        src_ref=xn6,
        dst_ref=x_res,
        send_sem=send_x.at[2, 0],
        recv_sem=recv_x.at[2, 0],
        device_id={"section": 1 - sec},
    )


    high, low = ctx // half, lax.rem(ctx, half)
    peers = []
    for far in range(half // 2, -1, -1):
        for other in (1, 0):
            for step in sorted({far, half - far if far else 0}):
                if (other, step) != (0, 0):
                    at = lax.rem(high + other, 2) * half + lax.rem(low + step, half)
                    peers.append((other * half + step, at))

    def exchange(phase, source, target):
        def send(d):
            return pltpu.make_async_remote_copy(
                src_ref=source(d),
                dst_ref=target(ctx),
                send_sem=send_c.at[phase, d],
                recv_sem=recv_c.at[phase, ctx],
                device_id={"ctx": d},
            )

        def arrival(d):
            return pltpu.make_async_remote_copy(
                src_ref=target(d),
                dst_ref=target(d),
                send_sem=send_c.at[phase, d],
                recv_sem=recv_c.at[phase, d],
                device_id={"ctx": d},
            )

        def start_all():
            for _, d in peers:
                send(d).start()

        def wait_all():
            for _, d in reversed(peers):
                arrival(d).wait_recv()

        def drain():
            for _, d in peers:
                send(d).wait_send()

        return send, start_all, wait_all, drain

    drains = []

    def enter():
        @pl.when(sec == 0)
        def _():
            pl.semaphore_wait(barrier, nc - 1 + nt - 1 + nt)

    @pl.when(sec == 1)
    def _():
        pl.semaphore_wait(barrier, nc - 1 + nt - 1 + nt)
        gain_copy.start()
        gain_copy.wait_send()


    def project(q):
        mine1, theirs1 = p1.at[q], r1.at[q]
        _, start, wait, drain = exchange(
            4 * q, lambda d: mine1.at[d], lambda d: theirs1.at[d]
        )
        drains.append(drain)

        @pl.when(sec == 1)
        def _():
            for j in range(q * owners, (q + 1) * owners):
                for copy in row_arrivals(j):
                    copy.wait_recv()

        here = pl.ds(q * owners, owners)
        xgv = xg[here].reshape(crows, model)
        squares = in_three(column_to_row(ssb[here].reshape(crows, LANES)))
        if q == 0:
            load_wq(tiles - 1).wait()
        kv = jnp.dot(xgv, wq_v[:, (tiles - 1) * 256 :], preferred_element_type=F32)
        for i in range(half):
            for part in range(2):
                block = kv[4 * i : 4 * i + 4, part * HD : (part + 1) * HD]
                mine1[part * half + i, pl.ds(crows, 8), :] = jnp.concatenate(
                    [block, squares[:4]], axis=0
                ).astype(BF16)
        for n in range(tiles - 1):
            if q == 0:
                load_wq(n).wait()
            two = jnp.dot(
                xgv, wq_v[:, n * 256 : n * 256 + 256], preferred_element_type=F32
            )
            mine1[2 * n, pl.ds(0, crows), :] = two[:, :HD].astype(BF16)
            mine1[2 * n + 1, pl.ds(0, crows), :] = two[:, HD:].astype(BF16)
        if q == 0:
            enter()
        start()
        theirs1[ctx] = mine1[ctx]
        return wait

    def spread(q, wait1):
        theirs1, mine2, theirs2 = r1.at[q], p2.at[q], r2.at[q]
        _, start, wait, drain = exchange(4 * q + 1, lambda d: mine2, lambda d: theirs2.at[d])
        drains.append(drain)
        wait1()
        total = theirs1[0].astype(F32)
        for d in range(1, nc):
            total = total + theirs1[d].astype(F32)
        square_row = jnp.sum(total[crows + 4 :], axis=0, keepdims=True)
        scale_row = lax.rsqrt(square_row / features + EPSILON)
        scale = row_to_column(scale_row, crows)
        picked = iota((8, LANES), 1) == iota((8, LANES), 0) + 4 * lax.rem(ctx, half)
        picked = picked & (iota((8, LANES), 0) < 4)
        kv_scale = jnp.sum(
            jnp.where(picked, jnp.broadcast_to(scale_row, (8, LANES)), 0.0),
            axis=1,
            keepdims=True,
        )
        done = jnp.concatenate(
            [total[:crows] * scale, total[crows:] * kv_scale], axis=0
        ).astype(BF16)
        mine2[...] = done
        theirs2[ctx] = done
        start()
        return wait

    block_rows = heads_at_once * crows
    blocks = heads // heads_at_once
    chunk = min(CHUNK, smax)
    stretch = min(STRETCH, prefix)
    all_rows = heads * crows
    first_block = blocks * ctx // nc

    def lane_max(best, values):
        for n in range(values.shape[1] // LANES):
            best = jnp.maximum(best, values[:, n * LANES : (n + 1) * LANES])
        return best

    def scores(queries, start, length):
        return lax.dot_general(
            queries,
            k_v[pl.ds(start, length), :],
            (((1,), (1,)), ((), ())),
            preferred_element_type=F32,
        )

    def attend(q, wait2):
        theirs2, mine3, theirs3 = r2.at[q], p3.at[q], r3.at[q]
        send, _, wait, drain = exchange(
            4 * q + 2, lambda d: mine3.at[d], lambda d: theirs3.at[d]
        )
        drains.append(drain)
        if q == 0:
            for copy in later:
                copy.wait()
        wait2()
        fresh_at = new_at + q * LANES
        for part, target in ((0, k_v), (1, vx)):
            fresh = [
                theirs2[part * half + i, pl.ds(crows, 8), :].astype(F32)[:4]
                for i in range(half)
            ]
            target[pl.ds(fresh_at, crows), pl.ds(0, HD)] = jnp.concatenate(
                fresh, axis=0
            ).astype(BF16)

        queries = theirs2[:, pl.ds(0, crows), :].reshape(all_rows, HD)
        best_v[...] = jnp.where(
            new_bias[...] == 0.0, scores(queries, fresh_at, LANES), NEGATIVE
        )
        s_v[:, new_at:] = best_v[...]

        def own_suffix(i, carry):
            best = best_v[...]
            held = order_v[q, :, 0:1] == slots * ctx + i
            filled = lengths[slots * ctx + i]
            base = pl.multiple_of(prefix + i * smax, smax)
            for n in range(smax // chunk):
                inside = iota((all_rows, chunk), 1) + n * chunk < filled
                at = pl.ds(base + n * chunk, chunk)
                values = scores(queries, base + n * chunk, chunk)
                values = jnp.where(held & inside, values, NEGATIVE)
                s_v[:, at] = values
                best = lane_max(best, values)
            best_v[...] = best
            return carry

        lax.fori_loop(0, slots, own_suffix, 0)

        def shared_prefix(i, carry):
            best = best_v[...]
            base = pl.multiple_of(i * stretch, stretch)
            for n in range(stretch // chunk):
                values = scores(queries, base + n * chunk, chunk)
                s_v[:, pl.ds(base + n * chunk, chunk)] = values
                best = lane_max(best, values)
            best_v[...] = best
            return carry

        lax.fori_loop(0, prefix // stretch, shared_prefix, 0)

        def one_block(b, carry):
            first = lax.rem(b + first_block, blocks) * heads_at_once
            here = pl.ds(pl.multiple_of(first * crows, block_rows), block_rows)
            top = jnp.max(best_v[here], axis=1, keepdims=True)
            sums = jnp.zeros((block_rows, 2 * HD), F32)
            for start in [n * chunk for n in range(new_at // chunk)] + [new_at]:
                length = chunk if start < new_at else LANES
                source = start if start < new_at else fresh_at
                weights = jnp.exp2((s_v[here, start : start + length] - top) * SCALE2)
                sums = sums + jnp.dot(
                    weights.astype(BF16),
                    vx[pl.ds(source, length), :],
                    preferred_element_type=F32,
                )
            weight_sum = sums[:, HD:]
            part = sums[:, :HD] / weight_sum
            level = top * SCALE2 + jnp.log2(weight_sum)
            for hh in range(heads_at_once):
                at = slice(hh * crows, (hh + 1) * crows)
                head = first + hh
                mine3[head] = jnp.concatenate(
                    [part[at], in_three(column_to_row(level[at]))], axis=0
                ).astype(BF16)

                @pl.when(head != ctx)
                def _():
                    send(head).start()

            return carry

        lax.fori_loop(0, blocks, one_block, 0)
        theirs3[ctx] = mine3[ctx]
        return wait

    def join(q, wait3):
        theirs3, mine4, theirs4 = r3.at[q], p4.at[q], a4.at[q]

        def columns(d):
            return theirs4.at[:, pl.ds(pl.multiple_of(d * HD, HD), HD)]

        _, start, wait, drain = exchange(4 * q + 3, lambda d: mine4, columns)
        drains.append(drain)
        wait3()
        levels = jnp.concatenate(
            [
                jnp.sum(theirs3[d, pl.ds(crows, 8), :].astype(F32), axis=0, keepdims=True)
                for d in range(nc)
            ],
            axis=0,
        )
        factors = jnp.exp2(levels - jnp.max(levels, axis=0, keepdims=True))
        factors = factors / jnp.sum(factors, axis=0, keepdims=True)
        padded = jnp.concatenate([factors, jnp.zeros((LANES - nc, LANES), F32)], axis=0)
        by_row = padded.T[:crows]
        joined = jnp.zeros((crows, HD), F32)
        for d in range(nc):
            joined = joined + by_row[:, d : d + 1] * theirs3[d, pl.ds(0, crows), :].astype(F32)
        attention = joined.astype(BF16)
        mine4[...] = attention
        theirs4[:, pl.ds(pl.multiple_of(ctx * HD, HD), HD)] = attention
        start()
        return wait

    def term_copy(d):
        return pltpu.make_async_remote_copy(
            src_ref=p5.at[slot(d)],
            dst_ref=r5.at[tp],
            send_sem=send_t.at[d],
            recv_sem=recv_t.at[tp],
            device_id={"tp": d},
        )

    def term_arrival(d):
        return pltpu.make_async_remote_copy(
            src_ref=r5.at[d],
            dst_ref=r5.at[d],
            send_sem=send_t.at[d],
            recv_sem=recv_t.at[d],
            device_id={"tp": d},
        )

    def start_terms(d):
        @pl.when(d != tp)
        def _():
            term_copy(d).start()

    def expand(q, wait4):
        if q == 0:
            out_load.wait()
        wait4()
        whole = a4[q]
        for n in range(width // 256):
            cols = slice(n * 256, n * 256 + 256)
            terms = jnp.dot(whole, wo_v[:, cols], preferred_element_type=F32)
            p5[pl.ds(q * owners, owners), :, cols] = terms.reshape(owners, 8, 256).astype(BF16)
        for d in range(q, nt, CHUNKS):
            start_terms(d)

        @pl.when(tp_chunk == q)
        def _():
            finish()

    def finish():
        r5[tp] = p5[tp_slot]

        @pl.when(sec == 1)
        def _():
            rest_copy.wait_recv()

        for k in range(1, nt):
            term_arrival(lax.rem(tp + k, nt)).wait_recv()
        passed = r5[0].astype(F32)
        for d in range(1, nt):
            passed = passed + r5[d].astype(F32)
        passed = passed + x_res[...]

        @pl.when(sec == 0)
        def _():
            gain_copy.wait_recv()
            xg6[...] = (passed * gain_next[...].astype(F32)).astype(BF16)
            total = jnp.sum(passed * passed, axis=1, keepdims=True)
            ss6[...] = jnp.broadcast_to(total, (8, LANES))
            xn6[...] = passed
            for k in range(nt):
                for copy in row_copies(lax.rem(tp + k, nt)):
                    copy.start()
            rest_copy.start()

        for t in range(STEPS):
            out[0, t] = passed[4 * t : 4 * t + 4]

    waits = [None] * CHUNKS
    for stage in (project, spread, attend, join, expand):
        for q in range(CHUNKS):
            waits[q] = stage(q) if stage is project else stage(q, waits[q])

    for drain in drains:
        drain()
    for d in range(nt):

        @pl.when(d != tp)
        def _():
            term_copy(d).wait_send()

    @pl.when(sec == 0)
    def _():
        for k in range(nt):
            for copy in row_copies(k):
                copy.wait_send()
        rest_copy.wait_send()


def on_device(nc, nt, tokens, gain, w_qkv, w_out, pre_k, pre_v, suf_k, suf_v, lengths, order):
    rows = 8 * nt
    model, wide = w_qkv.shape[1:]
    deep, width = w_out.shape[1:]
    prefix = pre_k.shape[2]
    slots, smax = suf_k.shape[2:4]
    crows = rows // CHUNKS
    new_at = prefix + slots * smax
    keys = new_at + CHUNKS * LANES
    all_rows = nc * crows
    vmem, dma = pltpu.VMEM, pltpu.SemaphoreType.DMA
    anywhere = pl.BlockSpec(memory_space=pl.ANY)
    scalars = pl.BlockSpec(memory_space=pltpu.SMEM)
    return pl.pallas_call(
        functools.partial(kernel, nc, nt),
        out_shape=jax.ShapeDtypeStruct((1, STEPS, rows // STEPS // nt, width), F32),
        in_specs=[anywhere] * 8 + [scalars] * 2,
        out_specs=pl.BlockSpec(memory_space=pltpu.VMEM),
        scratch_shapes=[
            vmem(tokens.shape, BF16),
            vmem((1, model), BF16),
            vmem((1, model), BF16),
            vmem((model, wide), BF16),
            vmem((deep, width), BF16),
            vmem((keys, HD), BF16),
            vmem((keys, 2 * HD), BF16),
            vmem((nt, 8, model), BF16),
            vmem((8, width), F32),
            vmem((nt, 8, LANES), F32),
            vmem((CHUNKS, nc, crows + 8, HD), BF16),
            vmem((CHUNKS, nc, crows + 8, HD), BF16),
            vmem((CHUNKS, crows + 8, HD), BF16),
            vmem((CHUNKS, nc, crows + 8, HD), BF16),
            vmem((CHUNKS, all_rows, LANES), jnp.int32),
            vmem((all_rows, LANES), F32),
            vmem((all_rows, new_at + LANES), F32),
            vmem((all_rows, LANES), F32),
            vmem((CHUNKS, nc, crows + 8, HD), BF16),
            vmem((CHUNKS, nc, crows + 8, HD), BF16),
            vmem((CHUNKS, crows, HD), BF16),
            vmem((CHUNKS, crows, nc * HD), BF16),
            vmem((nt, 8, width), BF16),
            vmem((nt, 8, width), BF16),
            vmem((8, width), BF16),
            vmem((8, LANES), F32),
            vmem((8, width), F32),
            dma((5 + 2 * slots,)),
            dma((wide // 256,)),
            dma((4 * CHUNKS, nc)),
            dma((4 * CHUNKS, nc)),
            dma((nt,)),
            dma((nt,)),
            dma((3, nt)),
            dma((3, nt)),
            dma,
            dma,
        ],
        compiler_params=pltpu.CompilerParams(
            collective_id=0, has_side_effects=True, vmem_limit_bytes=60 * 1024 * 1024
        ),
    )(tokens, gain, w_qkv, w_out, pre_k, pre_v, suf_k, suf_v, lengths, order)


def solution(mesh):
    nc, nt = mesh.shape["ctx"], mesh.shape["tp"]
    in_specs = (
        P(None, None, "ctx"),
        P("section", "ctx"),
        P("section", "ctx", "tp"),
        P("section", "tp", "ctx"),
        P("section", "tp", "ctx", None),
        P("section", "tp", "ctx", None),
        P("section", "tp", "ctx", None, None),
        P("section", "tp", "ctx", None, None),
        P(),
        P(),
    )
    return jax.shard_map(
        functools.partial(on_device, nc, nt),
        mesh=mesh,
        in_specs=in_specs,
        out_specs=P("section", None, "tp", "ctx"),
        check_vma=False,
    )
```

time: 131 us -> 105 us (0.80)
  Pallas kernels: 130 us -> 103 us
    pallas_call x1, Pallas kernels: 130 us -> 103 us  [on_device(): pl.pallas_call(functools.partial(kernel, nc, nt), out_shape=jax.ShapeDtyp...]
where the time goes in v2:
time: 105 us
  Pallas kernels  103 us (98%)
  local copies, waits for them, and re-layouts  1.38 us (1%)
    pallas_call x1, Pallas kernels, on_device(): pl.pallas_call(functools.partial(kernel, nc, nt), out_shape=jax.ShapeDtyp...  103 us

profile of v2, /device:TPU:3, one launch (start us, length us, event | category | flops | bytes accessed | tf_op | source)
XLA Modules:
  0.0 104.7 jit_solution(5719774757483632237)
XLA Ops:
  0.0 103.3 %shard_map.100 = f32[1,2,4,1024]{3,2,1,0:T(4,128)} custom-call(bf16[2,32,1024]{2,1,0:T(8,128)(2,1)} %tokens.1, bf16[1,1024]{1,0:T(2,128)(2,1)} %gain.1, bf16[1,1024,2304]{2,1,0:T(8,128)(2,1)} %w_qkv.1, bf16[1,2048,1024]{2,1,0:T(8,128)(2,1)} %w_out.1, bf16[1,1,4096,128]{3,2,1,0:T(8,128)(2,1)} %pre_keys.1, bf16[1,1,4096,128]{3,2,1,0:T(8,128)(2,1)} %pre_values.1, ...), custom_call_target="tpu_custom_call" | custom-call | tf_op jit(solution)/shard_map/pallas_call | solution.py:629
  103.3 1.4 %copy.12 = f32[1,2,4,1024]{3,2,1,0:T(4,128)} copy(f32[1,2,4,1024]{3,2,1,0:T(4,128)} %shard_map.100) | data formatting | bytes 65536

commit v3 on v2

v3 whole, which is shorter than its diff:
```python
import functools
import math

import jax
import jax.numpy as jnp
from jax import lax
from jax.experimental import pallas as pl
from jax.experimental.pallas import tpu as pltpu
from jax.sharding import PartitionSpec as P

HD = 128
LANES = 128
STEPS = 2
EPSILON = 1e-05
NEGATIVE = -1e30
SCALE2 = HD ** (-0.5) * math.log2(math.e)
CHUNKS = 2
CHUNK = 512
F32 = jnp.float32
BF16 = jnp.bfloat16


def iota(shape, dim):
    return lax.broadcasted_iota(jnp.int32, shape, dim)


def column_to_row(column):
    rows = column.shape[0]
    picked = jnp.where(iota((rows, LANES), 0) == iota((rows, LANES), 1), column, 0.0)
    return jnp.sum(picked, axis=0, keepdims=True)


def row_to_column(row, rows):
    spread = jnp.broadcast_to(row, (rows, LANES))
    picked = jnp.where(iota((rows, LANES), 0) == iota((rows, LANES), 1), spread, 0.0)
    return jnp.sum(picked, axis=1, keepdims=True)


def in_three(row):
    high = row.astype(BF16).astype(F32)
    rest = row - high
    middle = rest.astype(BF16).astype(F32)
    low = rest - middle
    which = iota((8, LANES), 0)
    block = jnp.where(which == 0, jnp.broadcast_to(high, (8, LANES)), 0.0)
    block = jnp.where(which == 1, jnp.broadcast_to(middle, (8, LANES)), block)
    return jnp.where(which == 2, jnp.broadcast_to(low, (8, LANES)), block)


def kernel(
    nc,
    nt,
    tokens,
    gain,
    w_qkv,
    w_out,
    pre_keys,
    pre_values,
    suf_keys,
    suf_values,
    lengths,
    order,
    out,
    tok_v,
    gain_v,
    wq_v,
    wo_v,
    k_v,
    vx,
    xg,
    x_res,
    ssb,
    p1,
    r1,
    p2,
    r2,
    order_v,
    new_bias,
    s_v,
    best_v,
    p3,
    r3,
    p4,
    a4,
    p5,
    r5,
    xg6,
    ss6,
    xn6,
    xn_back,
    load_sem,
    wq_sem,
    send_c,
    recv_c,
    send_t,
    recv_t,
    send_x,
    recv_x,
    send_g,
    recv_g,
):
    sec = lax.axis_index("section")
    tp = lax.axis_index("tp")
    ctx = lax.axis_index("ctx")
    rows = 8 * nt
    owners = nt // CHUNKS
    crows = rows // CHUNKS
    half = nc // 2
    heads = nc
    heads_at_once = half

    def slot(j):
        return j % CHUNKS * owners + j // CHUNKS

    tp_chunk = lax.rem(tp, CHUNKS)
    tp_slot = tp_chunk * owners + tp // CHUNKS
    model = wq_v.shape[0]
    prefix = pre_keys.shape[2]
    slots, smax = suf_keys.shape[2], suf_keys.shape[3]
    width = wo_v.shape[1]
    features = model * nc
    new_at = prefix + slots * smax
    tiles = wq_sem.shape[0]

    high, low = ctx // half, lax.rem(ctx, half)

    def from_afar(count):
        return sorted(range(count), key=lambda step: -min(step, count - step))

    peers = [
        (other, lax.rem(high + other, 2) * half + lax.rem(low + step, half))
        for step in from_afar(half)
        for other in (1, 0)
        if (other, step) != (0, 0)
    ]
    pairs = half // 2
    tile_order = [
        lax.rem(high + other, 2) * pairs + lax.rem(low // 2 + step, pairs)
        for step in from_afar(pairs)
        for other in (1, 0)
    ]

    def load(source, target, k):
        return pltpu.make_async_copy(source, target, load_sem.at[k])

    def load_wq(n):
        cols = pl.ds(pl.multiple_of(n * 256, 256), 256)
        return pltpu.make_async_copy(
            w_qkv.at[0, :, cols], wq_v.at[:, cols], wq_sem.at[n]
        )

    barrier = pltpu.get_barrier_semaphore()
    for _, d in peers:
        pl.semaphore_signal(barrier, inc=1, device_id={"ctx": d})
    for k in from_afar(nt)[:-1]:
        pl.semaphore_signal(barrier, inc=1, device_id={"tp": lax.rem(tp + k, nt)})
    for k in range(nt):
        pl.semaphore_signal(barrier, inc=1, device_id={"section": 1 - sec, "tp": k})

    loads = [
        load(tokens, tok_v, 0),
        load(gain, gain_v, 1),
    ]
    for copy in loads:
        copy.start()
    for n in [tiles - 1] + tile_order:
        load_wq(n).start()
    later = [
        load(pre_keys.at[0, 0], k_v.at[pl.ds(0, prefix)], 2),
        load(pre_values.at[0, 0], vx.at[pl.ds(0, prefix), pl.ds(0, HD)], 3),
    ]
    for i in range(slots):
        at = pl.ds(prefix + i * smax, smax)
        later.append(load(suf_keys.at[0, 0, i], k_v.at[at], 4 + 2 * i))
        later.append(load(suf_values.at[0, 0, i], vx.at[at, pl.ds(0, HD)], 5 + 2 * i))
    out_load = load(w_out.at[0], wo_v, 4 + 2 * slots)
    vx[:, HD:] = jnp.ones((vx.shape[0], HD), BF16)
    spare = LANES - 16
    for q in range(CHUNKS):
        at = pl.ds(new_at + q * LANES + 16, spare)
        k_v[at, :] = jnp.zeros((spare, HD), BF16)
        vx[at, pl.ds(0, HD)] = jnp.zeros((spare, HD), BF16)
    row_of = iota((crows, LANES), 0)
    lane_of = iota((crows, LANES), 1)
    batch_row = ((row_of >> 3) << 2) + (row_of & 3)
    second = (row_of & 4) == 4
    mine = batch_row == ctx
    allowed = mine & ((lane_of == 0) | (second & (lane_of == 1)))
    bias = jnp.where(allowed, 0.0, NEGATIVE)
    for q in range(CHUNKS):
        sample = jnp.zeros((crows, LANES), jnp.int32)
        for r in range(4 * owners):
            sample = jnp.where(batch_row == r, order[4 * (CHUNKS * (r // 4) + q) + r % 4], sample)
        for hh in range(heads_at_once):
            order_v[q, pl.ds(hh * crows, crows), :] = sample
    for hh in range(heads_at_once):
        new_bias[pl.ds(hh * crows, crows), :] = bias

    for copy in loads:
        copy.wait()

    def first_rows(j):
        return jnp.concatenate(
            [tok_v[t, pl.ds(4 * j, 4), :].astype(F32) for t in range(STEPS)], axis=0
        )

    @pl.when(sec == 0)
    def _():
        g = gain_v[...].astype(F32)
        for j in range(nt):
            x8 = first_rows(j)
            xg[slot(j)] = (x8 * g).astype(BF16)
            total = jnp.sum(x8 * x8, axis=1, keepdims=True)
            ssb[slot(j)] = jnp.broadcast_to(total, (8, LANES))

    def term_copy(q, step):
        place = lax.rem(tp // CHUNKS + step, owners)
        d = CHUNKS * place + q
        return d, pltpu.make_async_remote_copy(
            src_ref=p5.at[q * owners + place],
            dst_ref=r5.at[sec, tp],
            send_sem=send_t.at[d],
            recv_sem=recv_t.at[sec, tp],
            device_id={"section": 1, "tp": d},
        )

    def each_term(q, act):
        for step in from_afar(owners):
            d, copy = term_copy(q, step)

            @pl.when((sec == 0) | (d != tp))
            def _():
                act(copy)

    def term_arrival(layer, d):
        return pltpu.make_async_remote_copy(
            src_ref=r5.at[layer, d],
            dst_ref=r5.at[layer, d],
            send_sem=send_t.at[d],
            recv_sem=recv_t.at[layer, d],
            device_id={"section": 1, "tp": d},
        )

    def row_copies(k):
        return [
            pltpu.make_async_remote_copy(
                src_ref=source,
                dst_ref=target.at[tp_slot],
                send_sem=send_x.at[i, k],
                recv_sem=recv_x.at[i, tp_slot],
                device_id={"tp": k},
            )
            for i, (source, target) in enumerate(((xg6, xg), (ss6, ssb)))
        ]

    def row_arrivals(j):
        return [
            pltpu.make_async_remote_copy(
                src_ref=target.at[j],
                dst_ref=target.at[j],
                send_sem=send_x.at[i, j],
                recv_sem=recv_x.at[i, j],
                device_id={"tp": j},
            )
            for i, target in enumerate((xg, ssb))
        ]

    back_copy = pltpu.make_async_remote_copy(
        src_ref=xn6,
        dst_ref=xn_back,
        send_sem=send_g,
        recv_sem=recv_g,
        device_id={"section": 1 - sec},
    )

    def exchange(phase, source, target):
        def send(d):
            return pltpu.make_async_remote_copy(
                src_ref=source(d),
                dst_ref=target(ctx),
                send_sem=send_c.at[phase, d],
                recv_sem=recv_c.at[phase, ctx],
                device_id={"ctx": d},
            )

        def arrival(d):
            return pltpu.make_async_remote_copy(
                src_ref=target(d),
                dst_ref=target(d),
                send_sem=send_c.at[phase, d],
                recv_sem=recv_c.at[phase, d],
                device_id={"ctx": d},
            )

        def start_all():
            for _, d in peers:
                send(d).start()

        def wait_all(columns=(0, 1)):
            for other, d in reversed(peers):
                if other in columns:
                    arrival(d).wait_recv()

        def drain():
            for _, d in peers:
                send(d).wait_send()

        return send, start_all, wait_all, drain

    drains = []

    def enter():
        @pl.when(sec == 0)
        def _():
            pl.semaphore_wait(barrier, nc - 1 + nt - 1 + nt)

    @pl.when(sec == 1)
    def _():
        for j in range(nt):

            @pl.when(tp == j)
            def _():
                x_res[...] = first_rows(j)

        pl.semaphore_wait(barrier, nc - 1 + nt - 1 + nt)
        for k in range(nt):
            term_arrival(0, k).wait_recv()
        passed = r5[0, 0].astype(F32)
        for d in range(1, nt):
            passed = passed + r5[0, d].astype(F32)
        passed = passed + x_res[...]
        rows6 = (passed * gain_v[...].astype(F32)).astype(BF16)
        total = jnp.sum(passed * passed, axis=1, keepdims=True)
        squares6 = jnp.broadcast_to(total, (8, LANES))
        xg6[...] = rows6
        ss6[...] = squares6
        xn6[...] = passed
        for k in from_afar(nt)[:-1]:
            for copy in row_copies(lax.rem(tp + k, nt)):
                copy.start()
        back_copy.start()
        xg[tp_slot] = rows6
        ssb[tp_slot] = squares6


    def project(q):
        mine1, theirs1 = p1.at[q], r1.at[q]
        send, _, wait, drain = exchange(
            4 * q, lambda d: mine1.at[d], lambda d: theirs1.at[d]
        )
        drains.append(drain)

        @pl.when(sec == 1)
        def _():
            for j in range(q * owners, (q + 1) * owners):

                @pl.when(j != tp_slot)
                def _():
                    for copy in row_arrivals(j):
                        copy.wait_recv()

        here = pl.ds(q * owners, owners)
        xgv = xg[here].reshape(crows, model)
        squares = in_three(column_to_row(ssb[here].reshape(crows, LANES)))
        if q == 0:
            load_wq(tiles - 1).wait()
        kv = jnp.dot(xgv, wq_v[:, (tiles - 1) * 256 :], preferred_element_type=F32)
        for i in range(nc):
            first = i // 4 * 8 + i % 4
            block = [
                kv[first + 4 * t : first + 4 * t + 1, part * HD : (part + 1) * HD]
                for part in range(2)
                for t in range(STEPS)
            ]
            mine1[i, pl.ds(crows, 8), :] = jnp.concatenate(
                [*block, squares[:4]], axis=0
            ).astype(BF16)
        ready = []
        for n in tile_order:
            if q == 0:
                load_wq(n).wait()
            cols = pl.ds(pl.multiple_of(n * 256, 256), 256)
            two = jnp.dot(xgv, wq_v[:, cols], preferred_element_type=F32)
            mine1[2 * n, pl.ds(0, crows), :] = two[:, :HD].astype(BF16)
            mine1[2 * n + 1, pl.ds(0, crows), :] = two[:, HD:].astype(BF16)
            if len(ready) == 2:
                if q == 0:
                    enter()
            if len(ready) >= 2:
                send(ready[-2]).start()
                send(ready[-1]).start()
            ready += [2 * n, 2 * n + 1]
        if q == 0 and len(ready) <= 2:
            enter()
        for d in ready[-2:]:

            @pl.when(d != ctx)
            def _():
                send(d).start()

        theirs1[ctx] = mine1[ctx]
        if q == 0:
            for copy in later:
                copy.start()
            out_load.start()
        return wait

    def spread(q, wait1):
        theirs1, mine2, theirs2 = r1.at[q], p2.at[q], r2.at[q]
        _, start, wait, drain = exchange(4 * q + 1, lambda d: mine2, lambda d: theirs2.at[d])
        drains.append(drain)
        wait1()
        total = theirs1[0].astype(F32)
        for d in range(1, nc):
            total = total + theirs1[d].astype(F32)
        square_row = jnp.sum(total[crows + 4 :], axis=0, keepdims=True)
        scale_row = lax.rsqrt(square_row / features + EPSILON)
        scale = row_to_column(scale_row, crows)
        place = (ctx // 4) * 8 + lax.rem(ctx, 4) + 4 * (iota((8, LANES), 0) & 1)
        kv_scale = jnp.sum(
            jnp.where(
                iota((8, LANES), 1) == place, jnp.broadcast_to(scale_row, (8, LANES)), 0.0
            ),
            axis=1,
            keepdims=True,
        )
        done = (total[:crows] * scale).astype(BF16)
        mine2[...] = done
        theirs2[ctx] = done
        start()
        fresh = total[crows:] * kv_scale
        lines = iota((16, LANES), 0)
        for part, target in ((0, k_v), (1, vx)):
            both = jnp.where(
                lines == 0,
                jnp.broadcast_to(fresh[2 * part : 2 * part + 1], (16, LANES)),
                jnp.broadcast_to(fresh[2 * part + 1 : 2 * part + 2], (16, LANES)),
            )
            target[pl.ds(new_at + q * LANES, 16), pl.ds(0, HD)] = jnp.where(
                lines < 2, both, 0.0
            ).astype(BF16)
        return wait

    block_rows = heads_at_once * crows
    chunk = min(CHUNK, smax)
    all_rows = heads * crows

    def lane_max(best, values):
        for n in range(values.shape[1] // LANES):
            best = jnp.maximum(best, values[:, n * LANES : (n + 1) * LANES])
        return best

    def scores(queries, start, length):
        return lax.dot_general(
            queries,
            k_v[pl.ds(start, length), :],
            (((1,), (1,)), ((), ())),
            preferred_element_type=F32,
        )

    def attend(q, wait2):
        theirs2, mine3, theirs3 = r2.at[q], p3.at[q], r3.at[q]
        send, _, wait, drain = exchange(
            4 * q + 2, lambda d: mine3.at[d], lambda d: theirs3.at[d]
        )
        drains.append(drain)
        if q == 0:
            for copy in later:
                copy.wait()
        early = q < CHUNKS - 1
        if not early:
            wait2()

        def first_of(b):
            return lax.rem(b + high + (0 if early else 1), 2) * heads_at_once

        fresh_at = new_at + q * LANES

        def score_block(b, carry):
            if early:

                @pl.when(b == 0)
                def _():
                    wait2((0,))

                @pl.when(b == 1)
                def _():
                    wait2((1,))

            first = first_of(b)
            here = pl.ds(pl.multiple_of(first * crows, block_rows), block_rows)
            queries = theirs2[pl.ds(first, heads_at_once)]
            queries = queries.reshape(block_rows, HD)
            best = jnp.full((block_rows, LANES), NEGATIVE, F32)
            for n in range(prefix // chunk):
                values = scores(queries, n * chunk, chunk)
                s_v[here, n * chunk : (n + 1) * chunk] = values
                best = lane_max(best, values)
            for i in range(slots):
                held = order_v[q, :, 0:1] == slots * ctx + i
                filled = lengths[slots * ctx + i]
                for n in range(smax // chunk):
                    start = prefix + i * smax + n * chunk
                    inside = iota((block_rows, chunk), 1) + n * chunk < filled
                    values = scores(queries, start, chunk)
                    values = jnp.where(held & inside, values, NEGATIVE)
                    s_v[here, start : start + chunk] = values
                    best = lane_max(best, values)
            values = jnp.where(
                new_bias[...] == 0.0, scores(queries, fresh_at, LANES), NEGATIVE
            )
            s_v[here, new_at:] = values
            best_v[here] = jnp.maximum(best, values)

            @pl.when(sec >= 0)
            def _():
                weigh_block(first, here)

            return carry

        def weigh_block(first, here):
            top = jnp.max(best_v[here], axis=1, keepdims=True)
            sums = jnp.zeros((block_rows, 2 * HD), F32)
            for start in [n * chunk for n in range(new_at // chunk)] + [new_at]:
                length = chunk if start < new_at else LANES
                source = start if start < new_at else fresh_at
                weights = jnp.exp2((s_v[here, start : start + length] - top) * SCALE2)
                sums = sums + jnp.dot(
                    weights.astype(BF16),
                    vx[pl.ds(source, length), :],
                    preferred_element_type=F32,
                )
            weight_sum = sums[:, HD:]
            part = sums[:, :HD] / weight_sum
            level = top * SCALE2 + jnp.log2(weight_sum)
            for hh in range(heads_at_once):
                at = slice(hh * crows, (hh + 1) * crows)
                head = first + hh
                mine3[head] = jnp.concatenate(
                    [part[at], in_three(column_to_row(level[at]))], axis=0
                ).astype(BF16)
            for step in from_afar(half)[:-1]:
                send(first + lax.rem(low + step, half)).start()

            @pl.when(first + low != ctx)
            def _():
                send(first + low).start()

        lax.fori_loop(0, 2, score_block, 0)
        theirs3[ctx] = mine3[ctx]
        return wait

    def join(q, wait3):
        theirs3, mine4, theirs4 = r3.at[q], p4.at[q], a4.at[q]

        def columns(d):
            return theirs4.at[:, pl.ds(pl.multiple_of(d * HD, HD), HD)]

        _, start, wait, drain = exchange(4 * q + 3, lambda d: mine4, columns)
        drains.append(drain)
        wait3()
        levels = jnp.concatenate(
            [
                jnp.sum(theirs3[d, pl.ds(crows, 8), :].astype(F32), axis=0, keepdims=True)
                for d in range(nc)
            ],
            axis=0,
        )
        factors = jnp.exp2(levels - jnp.max(levels, axis=0, keepdims=True))
        factors = factors / jnp.sum(factors, axis=0, keepdims=True)
        padded = jnp.concatenate([factors, jnp.zeros((LANES - nc, LANES), F32)], axis=0)
        by_row = padded.T[:crows]
        joined = jnp.zeros((crows, HD), F32)
        for d in range(nc):
            joined = joined + by_row[:, d : d + 1] * theirs3[d, pl.ds(0, crows), :].astype(F32)
        attention = joined.astype(BF16)
        mine4[...] = attention
        theirs4[:, pl.ds(pl.multiple_of(ctx * HD, HD), HD)] = attention
        start()
        return wait

    def expand(q, wait4):
        if q == 0:
            out_load.wait()
        wait4()
        whole = a4[q]
        for n in range(width // 256):
            cols = slice(n * 256, n * 256 + 256)
            terms = jnp.dot(whole, wo_v[:, cols], preferred_element_type=F32)
            p5[pl.ds(q * owners, owners), :, cols] = terms.reshape(owners, 8, 256).astype(BF16)
        each_term(q, lambda copy: copy.start())

    def finish():
        @pl.when(sec == 0)
        def _():
            back_copy.wait_recv()
            for t in range(STEPS):
                out[0, t] = xn_back[4 * t : 4 * t + 4]

        @pl.when(sec == 1)
        def _():
            r5[1, tp] = p5[tp_slot]
            for k in from_afar(nt)[::-1][1:]:
                term_arrival(1, lax.rem(tp + k, nt)).wait_recv()
            passed = r5[1, 0].astype(F32)
            for d in range(1, nt):
                passed = passed + r5[1, d].astype(F32)
            passed = passed + xn6[...]
            for t in range(STEPS):
                out[0, t] = passed[4 * t : 4 * t + 4]

    waits = [None] * CHUNKS
    for stage in (project, spread, attend, join, expand):
        for q in range(CHUNKS):
            waits[q] = stage(q) if stage is project else stage(q, waits[q])

    for drain in drains:
        drain()
    finish()
    for q in range(CHUNKS):
        each_term(q, lambda copy: copy.wait_send())

    @pl.when(sec == 1)
    def _():
        for k in from_afar(nt)[:-1]:
            for copy in row_copies(lax.rem(tp + k, nt)):
                copy.wait_send()
        back_copy.wait_send()


def on_device(nc, nt, tokens, gain, w_qkv, w_out, pre_k, pre_v, suf_k, suf_v, lengths, order):
    rows = 8 * nt
    model, wide = w_qkv.shape[1:]
    deep, width = w_out.shape[1:]
    prefix = pre_k.shape[2]
    slots, smax = suf_k.shape[2:4]
    crows = rows // CHUNKS
    new_at = prefix + slots * smax
    keys = new_at + CHUNKS * LANES
    all_rows = nc * crows
    vmem, dma = pltpu.VMEM, pltpu.SemaphoreType.DMA
    anywhere = pl.BlockSpec(memory_space=pl.ANY)
    scalars = pl.BlockSpec(memory_space=pltpu.SMEM)
    return pl.pallas_call(
        functools.partial(kernel, nc, nt),
        out_shape=jax.ShapeDtypeStruct((1, STEPS, rows // STEPS // nt, width), F32),
        in_specs=[anywhere] * 8 + [scalars] * 2,
        out_specs=pl.BlockSpec(memory_space=pltpu.VMEM),
        scratch_shapes=[
            vmem(tokens.shape, BF16),
            vmem((1, model), BF16),
            vmem((model, wide), BF16),
            vmem((deep, width), BF16),
            vmem((keys, HD), BF16),
            vmem((keys, 2 * HD), BF16),
            vmem((nt, 8, model), BF16),
            vmem((8, width), F32),
            vmem((nt, 8, LANES), F32),
            vmem((CHUNKS, nc, crows + 8, HD), BF16),
            vmem((CHUNKS, nc, crows + 8, HD), BF16),
            vmem((CHUNKS, crows, HD), BF16),
            vmem((CHUNKS, nc, crows, HD), BF16),
            vmem((CHUNKS, all_rows // 2, LANES), jnp.int32),
            vmem((all_rows // 2, LANES), F32),
            vmem((all_rows, new_at + LANES), F32),
            vmem((all_rows, LANES), F32),
            vmem((CHUNKS, nc, crows + 8, HD), BF16),
            vmem((CHUNKS, nc, crows + 8, HD), BF16),
            vmem((CHUNKS, crows, HD), BF16),
            vmem((CHUNKS, crows, nc * HD), BF16),
            vmem((nt, 8, width), BF16),
            vmem((2, nt, 8, width), BF16),
            vmem((8, width), BF16),
            vmem((8, LANES), F32),
            vmem((8, width), F32),
            vmem((8, width), F32),
            dma((5 + 2 * slots,)),
            dma((wide // 256,)),
            dma((4 * CHUNKS, nc)),
            dma((4 * CHUNKS, nc)),
            dma((nt,)),
            dma((2, nt)),
            dma((2, nt)),
            dma((2, nt)),
            dma,
            dma,
        ],
        compiler_params=pltpu.CompilerParams(
            collective_id=0, has_side_effects=True, vmem_limit_bytes=60 * 1024 * 1024
        ),
    )(tokens, gain, w_qkv, w_out, pre_k, pre_v, suf_k, suf_v, lengths, order)


def solution(mesh):
    nc, nt = mesh.shape["ctx"], mesh.shape["tp"]
    in_specs = (
        P(None, None, "ctx"),
        P("section", "ctx"),
        P("section", "ctx", "tp"),
        P("section", "tp", "ctx"),
        P("section", "tp", "ctx", None),
        P("section", "tp", "ctx", None),
        P("section", "tp", "ctx", None, None),
        P("section", "tp", "ctx", None, None),
        P(),
        P(),
    )
    return jax.shard_map(
        functools.partial(on_device, nc, nt),
        mesh=mesh,
        in_specs=in_specs,
        out_specs=P("section", None, "tp", "ctx"),
        check_vma=False,
    )
```

time: 105 us -> 92.9 us (0.88)
  Pallas kernels: 103 us -> 91.1 us
    pallas_call x1, Pallas kernels: 103 us -> 91.1 us  [on_device(): pl.pallas_call(functools.partial(kernel, nc, nt), out_shape=jax.ShapeDtyp...]
where the time goes in v3:
time: 92.9 us; the launch traced here: 92.5 us
  Pallas kernels  91.1 us (98%)
  local copies, waits for them, and re-layouts  1.38 us (1%)
    pallas_call x1, Pallas kernels, on_device(): pl.pallas_call(functools.partial(kernel, nc, nt), out_shape=jax.ShapeDtyp...  91.1 us

profile of v3, /device:TPU:3, one launch (start us, length us, event | category | flops | bytes accessed | tf_op | source)
XLA Modules:
  0.0 92.5 jit_solution(11144236563067137824)
XLA Ops:
  0.0 91.1 %shard_map.100 = f32[1,2,4,1024]{3,2,1,0:T(4,128)} custom-call(bf16[2,32,1024]{2,1,0:T(8,128)(2,1)} %tokens.1, bf16[1,1024]{1,0:T(2,128)(2,1)} %gain.1, bf16[1,1024,2304]{2,1,0:T(8,128)(2,1)} %w_qkv.1, bf16[1,2048,1024]{2,1,0:T(8,128)(2,1)} %w_out.1, bf16[1,1,4096,128]{3,2,1,0:T(8,128)(2,1)} %pre_keys.1, bf16[1,1,4096,128]{3,2,1,0:T(8,128)(2,1)} %pre_values.1, ...), custom_call_target="tpu_custom_call" | custom-call | tf_op jit(solution)/shard_map/pallas_call | solution.py:644
  91.1 1.4 %copy.12 = f32[1,2,4,1024]{3,2,1,0:T(4,128)} copy(f32[1,2,4,1024]{3,2,1,0:T(4,128)} %shard_map.100) | data formatting | bytes 65536
